TPU v7x, 32 devices: a whole 2x2x4 slice. The times are simulated.
32 devices in a mesh: tm: 4 (over x, core), space: 8 (over z, y).
Axes of the slice: x: 2, y: 2, z: 4, core: 2. Of those that a mesh axis runs over, the one named last changes fastest.
Arguments:
- start_value: float32 [4, 8, 512, 256], P('tm', 'space'), may hold values from -6 to 6
- old_nodes: float32 [4, 3, 8, 512, 256], P('tm', None, 'space'), may hold values from -6 to 6
- diffusivity: float32 [8, 512, 256], P('space'), may hold values from 0.2 to 2
Outputs:
- fine_nodes: float32 [4, 3, 8, 512, 256], P('tm', None, 'space')
- next_start: float32 [4, 8, 512, 256], P('tm', 'space')
- next_coarse: float32 [4, 8, 512, 256], P('tm', 'space')
All inputs are finite; a program needn't handle non-finite values.
Results may differ from a plain program's by a relative error of at most 0.0001.
Values sent between devices are 32-bit elements; how exact they have to be, the bound alone decides.
No kernel may reach another device: no remote copies, remote signals or barrier semaphores. Data moves between devices by JAX's collectives and lax.ppermute only.
A program may use at most 64 MiB of HBM per device.

v0:
```python
import math

import jax
import jax.numpy as jnp
from jax import lax
from jax.sharding import PartitionSpec as P

CG_ITERS = 2


STEP = 2.0
ROOT_SIX = math.sqrt(6.0)
NODE_TIMES = [(4.0 - ROOT_SIX) / 10.0, (4.0 + ROOT_SIX) / 10.0, 1.0]
COLLOC = [
    [
        (88.0 - 7.0 * ROOT_SIX) / 360.0,
        (296.0 - 169.0 * ROOT_SIX) / 1800.0,
        (-2.0 + 3.0 * ROOT_SIX) / 225.0,
    ],
    [
        (296.0 + 169.0 * ROOT_SIX) / 1800.0,
        (88.0 + 7.0 * ROOT_SIX) / 360.0,
        (-2.0 - 3.0 * ROOT_SIX) / 225.0,
    ],
    [(16.0 - ROOT_SIX) / 36.0, (16.0 + ROOT_SIX) / 36.0, 1.0 / 9.0],
]


def padded_2(value, sides, width):
    for axis, dim in sides:
        devices, length = (lax.axis_size(axis), value.shape[dim])
        up = [(i, (i + 1) % devices) for i in range(devices - 1)]
        down = [(j, i) for i, j in up]
        last = lax.slice_in_dim(value, length - width, length, axis=dim)
        leading = lax.slice_in_dim(value, 0, width, axis=dim)
        before = lax.ppermute(last, axis, up)
        after = lax.ppermute(leading, axis, down)
        value = jnp.concatenate([before, value, after], axis=dim)
    return value


def from_behind(block, axis, distance):
    devices = range(lax.axis_size(axis))
    route = [(i - distance, i) for i in devices if i - distance in devices]
    return lax.ppermute(block, axis, route)


def sweep_weight(row, column):
    below = COLLOC[row - 1][column] if row > 0 else 0.0
    return COLLOC[row][column] - below


def node_width(row):
    below = NODE_TIMES[row - 1] if row > 0 else 0.0
    return NODE_TIMES[row] - below


def neighbour(field, dim, forward):
    length = field.shape[dim]
    edge = jnp.zeros_like(lax.slice_in_dim(field, 0, 1, axis=dim))
    if forward:
        return jnp.concatenate([lax.slice_in_dim(field, 1, length, axis=dim), edge], axis=dim)
    return jnp.concatenate([edge, lax.slice_in_dim(field, 0, length - 1, axis=dim)], axis=dim)


def combine(weights, images):
    summed = weights[0] * images[0]
    for column in range(1, 3):
        summed = summed + weights[column] * images[column]
    return summed


def inner(left, right):
    return jnp.sum(left * right, axis=(1, 2, 3))


def widen(values):
    return values[:, None, None, None]


def paired(residual, image):
    return lax.psum((inner(residual, residual), inner(residual, image)), "space")


def solve(guess, residual, widths, heat):
    width_grid = widen(widths)
    iterate = guess
    image = residual - width_grid * heat(residual)
    norm_now, product_sum = paired(residual, image)
    step_size = norm_now / product_sum
    direction = residual
    along_image = image
    for sweep in range(CG_ITERS):
        iterate = iterate + widen(step_size) * direction
        if sweep + 1 < CG_ITERS:
            residual = residual - widen(step_size) * along_image
            image = residual - width_grid * heat(residual)
            norm_next, product_sum = paired(residual, image)
            momentum = norm_next / norm_now
            step_size = norm_next / (product_sum - momentum * norm_next / step_size)
            direction = residual + widen(momentum) * direction
            along_image = image + widen(momentum) * along_image
            norm_now = norm_next
    return iterate


def on_device(start_value, old_nodes, diffusivity):
    padded_kappa = padded_2(diffusivity, (("space", 0),), 1)
    kappa_after = padded_kappa[2:]
    kappa_before = padded_kappa[:-2]

    def heat(stacked):
        padded = padded_2(stacked, (("space", 1),), 1)
        face_one = 0.5 * (diffusivity + kappa_after)
        face_two = 0.5 * (diffusivity + kappa_before)
        face_three = 0.5 * (diffusivity + neighbour(diffusivity, 1, True))
        face_four = 0.5 * (diffusivity + neighbour(diffusivity, 1, False))
        face_five = 0.5 * (diffusivity + neighbour(diffusivity, 2, True))
        face_six = 0.5 * (diffusivity + neighbour(diffusivity, 2, False))
        total = face_one + face_two + face_three + face_four + face_five + face_six
        result = face_one * padded[:, 2:] + face_two * padded[:, :-2]
        result = (
            result
            + face_three * neighbour(stacked, 2, True)
            + face_four * neighbour(stacked, 2, False)
        )
        result = (
            result
            + face_five * neighbour(stacked, 3, True)
            + face_six * neighbour(stacked, 3, False)
        )
        return result - total * stacked

    previous_nodes = old_nodes[0]
    begin = start_value[0]
    images = heat(previous_nodes)

    def fine_residual(row, previous):
        weights = [sweep_weight(row, column) for column in range(3)]
        return previous - previous_nodes[row] + STEP * combine(weights, images)

    coarse_res = begin - previous_nodes[2] + STEP * combine(COLLOC[2], images)
    first_res = fine_residual(0, begin)
    fresh = [
        solve(
            previous_nodes[0:1],
            first_res[None],
            jnp.array([STEP * node_width(0)], jnp.float32),
            heat,
        )[0]
    ]
    coarse_end = None
    for row in range(1, 3):
        residual = fine_residual(row, fresh[row - 1])
        result = solve(
            previous_nodes[row : row + 1],
            residual[None],
            jnp.array([STEP * node_width(row)], jnp.float32),
            heat,
        )
        fresh.append(result[0])
    coarse_end = solve(previous_nodes[2:3], coarse_res[None], jnp.array([STEP], jnp.float32), heat)[
        0
    ]
    moved = from_behind(jnp.stack([fresh[2], coarse_end]), "tm", 1)
    first_slice = lax.axis_index("tm") == 0
    next_start = jnp.where(first_slice, begin, moved[0])[None]
    next_coarse = jnp.where(first_slice, begin, moved[1])[None]
    return (jnp.stack(fresh)[None], next_start, next_coarse)


def solution(mesh):
    in_specs = (
        P("tm", "space", None, None),
        P("tm", None, "space", None, None),
        P("space", None, None),
    )
    out_specs = (
        P("tm", None, "space", None, None),
        P("tm", "space", None, None),
        P("tm", "space", None, None),
    )
    return jax.shard_map(
        on_device, mesh=mesh, in_specs=in_specs, out_specs=out_specs, check_vma=False
    )
```

profile of v0, /device:TPU:2, one launch (start us, length us, event | category | flops | bytes accessed | tf_op | source)
XLA Modules:
  0.0 452.3 jit_solution(13187722062762523463)
XLA Ops:
  2.1 4.6 %collective-permute-start.3 = (f32[3,1,512,256]{3,2,1,0:T(8,128)}, f32[3,1,512,256]{3,2,1,0:T(8,128)S(1)}, u32[]{:S(2)}, u32[]{:S(2)}) collective-permute-start(f32[3,1,512,256]{3,2,1,0:T(8,128)} %bitcast.385), channel_id=1, source_target_pairs={{0,1},{1,2},{2,3},{3,4},{4,5},{5,6},{6,7},{8,9},{9,10},{10,11},{11... | collective-permute-start | bytes 4718600 | tf_op jit(solution)/shard_map/ppermute | solution.py:36
  8.0 4.9 %collective-permute-start.2 = (f32[1,512,256]{2,1,0:T(8,128)}, f32[1,512,256]{2,1,0:T(8,128)S(1)}, u32[]{:S(2)}, u32[]{:S(2)}) collective-permute-start(f32[1,512,256]{2,1,0:T(8,128)} %param.9), channel_id=1, source_target_pairs={{0,1},{1,2},{2,3},{3,4},{4,5},{5,6},{6,7},{8,9},{9,10},{10,11},{11... | collective-permute-start | bytes 1572872 | tf_op jit(solution)/shard_map/ppermute | solution.py:36
  16.0 34.3 %collective-permute-done = f32[1,512,256]{2,1,0:T(8,128)S(1)} collective-permute-done((f32[1,512,256]{2,1,0:T(8,128)}, f32[1,512,256]{2,1,0:T(8,128)S(1)}, u32[]{:S(2)}, u32[]{:S(2)}) %collective-permute-start) | collective-permute-done | bytes 524320 | tf_op jit(solution)/shard_map/ppermute | solution.py:37
  50.2 45.0 %collective-permute-done.2 = f32[1,512,256]{2,1,0:T(8,128)S(1)} collective-permute-done((f32[1,512,256]{2,1,0:T(8,128)}, f32[1,512,256]{2,1,0:T(8,128)S(1)}, u32[]{:S(2)}, u32[]{:S(2)}) %collective-permute-start.2) | collective-permute-done | bytes 524320 | tf_op jit(solution)/shard_map/ppermute | solution.py:36
  100.0 4.9 %collective-permute-start.5 = (f32[1,1,512,256]{3,2,1,0:T(8,128)S(1)}, f32[1,1,512,256]{3,2,1,0:T(8,128)S(1)}, u32[]{:S(2)}, u32[]{:S(2)}) collective-permute-start(f32[1,1,512,256]{3,2,1,0:T(8,128)S(1)} %get-tuple-element.51), channel_id=1, source_target_pairs={{0,1},{1,2},{2,3},{3,4},{4,5},{5,6},{6,7},{8,9},{9,10},{10,11},{11... | collective-permute-start | bytes 1572872 | tf_op jit(solution)/shard_map/ppermute | solution.py:36
  106.3 6.2 %collective-permute-start.17 = (f32[1,1,512,256]{3,2,1,0:T(8,128)}, f32[1,1,512,256]{3,2,1,0:T(8,128)}, u32[]{:S(2)}, u32[]{:S(2)}) collective-permute-start(f32[1,1,512,256]{3,2,1,0:T(8,128)} %get-tuple-element.50), channel_id=1, source_target_pairs={{0,1},{1,2},{2,3},{3,4},{4,5},{5,6},{6,7},{8,9},{9,10},{10,11},{11... | collective-permute-start | bytes 1572872 | tf_op jit(solution)/shard_map/ppermute | solution.py:36
  117.2 20.6 %collective-permute-done.5 = f32[1,1,512,256]{3,2,1,0:T(8,128)S(1)} collective-permute-done((f32[1,1,512,256]{3,2,1,0:T(8,128)S(1)}, f32[1,1,512,256]{3,2,1,0:T(8,128)S(1)}, u32[]{:S(2)}, u32[]{:S(2)}) %collective-permute-start.5) | collective-permute-done | bytes 524320 | tf_op jit(solution)/shard_map/ppermute | solution.py:36
  139.9 22.2 %all-reduce.45 = (f32[1]{0:T(128)}, f32[1]{0:T(128)}) all-reduce(f32[1]{0:T(128)} %bitcast.9, f32[1]{0:T(128)} %bitcast.17), channel_id=1, replica_groups=mesh['tm'=4,'space'=8] {'space'}, use_global_device_ids=true, to_apply=%region_1.0 | all-reduce | flops 2 | bytes 16 | tf_op jit(solution)/shard_map/psum | solution.py:82
  178.0 7.7 %collective-permute-done.7 = f32[1,1,512,256]{3,2,1,0:T(8,128)S(1)} collective-permute-done((f32[1,1,512,256]{3,2,1,0:T(8,128)S(1)}, f32[1,1,512,256]{3,2,1,0:T(8,128)S(1)}, u32[]{:S(2)}, u32[]{:S(2)}) %collective-permute-start.7) | collective-permute-done | bytes 524320 | tf_op jit(solution)/shard_map/ppermute | solution.py:36
  186.9 21.5 %all-reduce.44 = (f32[1]{0:T(128)}, f32[1]{0:T(128)}) all-reduce(f32[1]{0:T(128)} %bitcast.19, f32[1]{0:T(128)} %bitcast.20), channel_id=1, replica_groups=mesh['tm'=4,'space'=8] {'space'}, use_global_device_ids=true, to_apply=%region_5.0 | all-reduce | flops 2 | bytes 16 | tf_op jit(solution)/shard_map/psum | solution.py:82
  221.7 4.9 %collective-permute-done.8 = f32[1,1,512,256]{3,2,1,0:T(8,128)S(1)} collective-permute-done((f32[1,1,512,256]{3,2,1,0:T(8,128)S(1)}, f32[1,1,512,256]{3,2,1,0:T(8,128)S(1)}, u32[]{:S(2)}, u32[]{:S(2)}) %collective-permute-start.8) | collective-permute-done | bytes 524320 | tf_op jit(solution)/shard_map/ppermute | solution.py:37
  226.7 8.8 %collective-permute-done.9 = f32[1,1,512,256]{3,2,1,0:T(8,128)S(1)} collective-permute-done((f32[1,1,512,256]{3,2,1,0:T(8,128)S(1)}, f32[1,1,512,256]{3,2,1,0:T(8,128)S(1)}, u32[]{:S(2)}, u32[]{:S(2)}) %collective-permute-start.9) | collective-permute-done | bytes 524320 | tf_op jit(solution)/shard_map/ppermute | solution.py:36
  237.5 20.3 %all-reduce.43 = (f32[1]{0:T(128)}, f32[1]{0:T(128)}) all-reduce(f32[1]{0:T(128)} %bitcast.24, f32[1]{0:T(128)} %bitcast.25), channel_id=1, replica_groups=mesh['tm'=4,'space'=8] {'space'}, use_global_device_ids=true, to_apply=%region_9.0 | all-reduce | flops 2 | bytes 16 | tf_op jit(solution)/shard_map/psum | solution.py:82
  266.6 5.5 %collective-permute-done.10 = f32[1,1,512,256]{3,2,1,0:T(8,128)S(1)} collective-permute-done((f32[1,1,512,256]{3,2,1,0:T(8,128)S(1)}, f32[1,1,512,256]{3,2,1,0:T(8,128)S(1)}, u32[]{:S(2)}, u32[]{:S(2)}) %collective-permute-start.10) | collective-permute-done | bytes 524320 | tf_op jit(solution)/shard_map/ppermute | solution.py:37
  272.1 8.9 %collective-permute-done.11 = f32[1,1,512,256]{3,2,1,0:T(8,128)S(1)} collective-permute-done((f32[1,1,512,256]{3,2,1,0:T(8,128)S(1)}, f32[1,1,512,256]{3,2,1,0:T(8,128)S(1)}, u32[]{:S(2)}, u32[]{:S(2)}) %collective-permute-start.11) | collective-permute-done | bytes 524320 | tf_op jit(solution)/shard_map/ppermute | solution.py:36
  282.2 20.3 %all-reduce.42 = (f32[1]{0:T(128)}, f32[1]{0:T(128)}) all-reduce(f32[1]{0:T(128)} %bitcast.27, f32[1]{0:T(128)} %bitcast.28), channel_id=1, replica_groups=mesh['tm'=4,'space'=8] {'space'}, use_global_device_ids=true, to_apply=%region_13.0 | all-reduce | flops 2 | bytes 16 | tf_op jit(solution)/shard_map/psum | solution.py:82
  315.8 5.8 %collective-permute-done.12 = f32[1,1,512,256]{3,2,1,0:T(8,128)S(1)} collective-permute-done((f32[1,1,512,256]{3,2,1,0:T(8,128)S(1)}, f32[1,1,512,256]{3,2,1,0:T(8,128)S(1)}, u32[]{:S(2)}, u32[]{:S(2)}) %collective-permute-start.12) | collective-permute-done | bytes 524320 | tf_op jit(solution)/shard_map/ppermute | solution.py:37
  321.6 9.2 %collective-permute-done.13 = f32[1,1,512,256]{3,2,1,0:T(8,128)S(1)} collective-permute-done((f32[1,1,512,256]{3,2,1,0:T(8,128)S(1)}, f32[1,1,512,256]{3,2,1,0:T(8,128)S(1)}, u32[]{:S(2)}, u32[]{:S(2)}) %collective-permute-start.13) | collective-permute-done | bytes 524320 | tf_op jit(solution)/shard_map/ppermute | solution.py:36
  332.8 20.3 %all-reduce.41 = (f32[1]{0:T(128)}, f32[1]{0:T(128)}, f32[1]{0:T(128)}, f32[1]{0:T(128)}) all-reduce(f32[1]{0:T(128)} %bitcast.32, f32[1]{0:T(128)} %bitcast.33, f32[1]{0:T(128)} %bitcast.40, f32[1]{0:T(128)} %bitcast.41), channel_id=1, replica_groups=mesh['tm'=4,'space'=8] {'space'}, use_global_device_ids=true, to_apply=%region_17.0 | all-reduce | flops 4 | bytes 32 | tf_op jit(solution)/shard_map/psum | solution.py:82
  359.0 4.8 %collective-permute-start.19 = (f32[1,1,512,256]{3,2,1,0:T(8,128)S(1)}, f32[1,1,512,256]{3,2,1,0:T(8,128)S(1)}, u32[]{:S(2)}, u32[]{:S(2)}) collective-permute-start(f32[1,1,512,256]{3,2,1,0:T(8,128)S(1)} %get-tuple-element.96), channel_id=1, source_target_pairs={{0,1},{1,2},{2,3},{3,4},{4,5},{5,6},{6,7},{8,9},{9,10},{10,11},{11... | collective-permute-start | bytes 1572872 | tf_op jit(solution)/shard_map/ppermute | solution.py:36
  374.4 15.8 %collective-permute-done.19 = f32[1,1,512,256]{3,2,1,0:T(8,128)S(1)} collective-permute-done((f32[1,1,512,256]{3,2,1,0:T(8,128)S(1)}, f32[1,1,512,256]{3,2,1,0:T(8,128)S(1)}, u32[]{:S(2)}, u32[]{:S(2)}) %collective-permute-start.19) | collective-permute-done | bytes 524320 | tf_op jit(solution)/shard_map/ppermute | solution.py:36
  391.5 9.9 %collective-permute-done.15 = f32[1,1,512,256]{3,2,1,0:T(8,128)S(1)} collective-permute-done((f32[1,1,512,256]{3,2,1,0:T(8,128)S(1)}, f32[1,1,512,256]{3,2,1,0:T(8,128)S(1)}, u32[]{:S(2)}, u32[]{:S(2)}) %collective-permute-start.15) | collective-permute-done | bytes 524320 | tf_op jit(solution)/shard_map/ppermute | solution.py:36
  402.5 20.3 %all-reduce.40 = (f32[1]{0:T(128)}, f32[1]{0:T(128)}, f32[1]{0:T(128)}, f32[1]{0:T(128)}) all-reduce(f32[1]{0:T(128)} %bitcast.35, f32[1]{0:T(128)} %bitcast.36, f32[1]{0:T(128)} %bitcast.43, f32[1]{0:T(128)} %bitcast.44), channel_id=1, replica_groups=mesh['tm'=4,'space'=8] {'space'}, use_global_device_ids=true, to_apply=%region_21.0 | all-reduce | flops 4 | bytes 32 | tf_op jit(solution)/shard_map/psum | solution.py:82
  438.1 13.1 %collective-permute-done.20 = f32[2,1,512,256]{3,2,1,0:T(8,128)S(1)} collective-permute-done((f32[2,1,512,256]{3,2,1,0:T(8,128)}, f32[2,1,512,256]{3,2,1,0:T(8,128)S(1)}, u32[]{:S(2)}, u32[]{:S(2)}) %collective-permute-start.20) | collective-permute-done | bytes 1048608 | tf_op jit(solution)/shard_map/ppermute | solution.py:45
  (136 shorter events, 87.9 us)
Async XLA Ops:
  0.6 95.0 %collective-permute-start.1 = (f32[3,1,512,256]{3,2,1,0:T(8,128)}, f32[3,1,512,256]{3,2,1,0:T(8,128)S(1)}, u32[]{:S(2)}, u32[]{:S(2)}) collective-permute-start(f32[3,1,512,256]{3,2,1,0:T(8,128)} %bitcast.384), channel_id=1, source_target_pairs={{1,0},{2,1},{3,2},{4,3},{5,4},{6,5},{7,6},{9,8},{10,9},{11,10},{12... | collective-permute-start | bytes 4718600 | tf_op jit(solution)/shard_map/ppermute | solution.py:37
  2.1 93.6 %collective-permute-start.3 = (f32[3,1,512,256]{3,2,1,0:T(8,128)}, f32[3,1,512,256]{3,2,1,0:T(8,128)S(1)}, u32[]{:S(2)}, u32[]{:S(2)}) collective-permute-start(f32[3,1,512,256]{3,2,1,0:T(8,128)} %bitcast.385), channel_id=1, source_target_pairs={{0,1},{1,2},{2,3},{3,4},{4,5},{5,6},{6,7},{8,9},{9,10},{10,11},{11... | collective-permute-start | bytes 4718600 | tf_op jit(solution)/shard_map/ppermute | solution.py:36
  6.7 43.5 %collective-permute-start = (f32[1,512,256]{2,1,0:T(8,128)}, f32[1,512,256]{2,1,0:T(8,128)S(1)}, u32[]{:S(2)}, u32[]{:S(2)}) collective-permute-start(f32[1,512,256]{2,1,0:T(8,128)} %param.9), channel_id=1, source_target_pairs={{1,0},{2,1},{3,2},{4,3},{5,4},{6,5},{7,6},{9,8},{10,9},{11,10},{12... | collective-permute-start | bytes 1572872 | tf_op jit(solution)/shard_map/ppermute | solution.py:37
  8.0 87.2 %collective-permute-start.2 = (f32[1,512,256]{2,1,0:T(8,128)}, f32[1,512,256]{2,1,0:T(8,128)S(1)}, u32[]{:S(2)}, u32[]{:S(2)}) collective-permute-start(f32[1,512,256]{2,1,0:T(8,128)} %param.9), channel_id=1, source_target_pairs={{0,1},{1,2},{2,3},{3,4},{4,5},{5,6},{6,7},{8,9},{9,10},{10,11},{11... | collective-permute-start | bytes 1572872 | tf_op jit(solution)/shard_map/ppermute | solution.py:36
  95.6 42.2 %copy-start.1 = (f32[1,512,256]{2,1,0:T(8,128)}, f32[1,512,256]{2,1,0:T(8,128)S(1)}, u32[]{:S(2)}) copy-start(f32[1,512,256]{2,1,0:T(8,128)S(1)} %get-tuple-element.47) | copy-start | bytes 1572868
  95.6 42.2 %copy-start.7 = (f32[1,512,256]{2,1,0:T(8,128)}, f32[1,512,256]{2,1,0:T(8,128)S(1)}, u32[]{:S(2)}) copy-start(f32[1,512,256]{2,1,0:T(8,128)S(1)} %get-tuple-element.48) | copy-start | bytes 1572868
  98.7 18.5 %collective-permute-start.4 = (f32[1,1,512,256]{3,2,1,0:T(8,128)S(1)}, f32[1,1,512,256]{3,2,1,0:T(8,128)S(1)}, u32[]{:S(2)}, u32[]{:S(2)}) collective-permute-start(f32[1,1,512,256]{3,2,1,0:T(8,128)S(1)} %get-tuple-element.51), channel_id=1, source_target_pairs={{1,0},{2,1},{3,2},{4,3},{5,4},{6,5},{7,6},{9,8},{10,9},{11,10},{12... | collective-permute-start | bytes 1572872 | tf_op jit(solution)/shard_map/ppermute | solution.py:37
  100.0 37.8 %collective-permute-start.5 = (f32[1,1,512,256]{3,2,1,0:T(8,128)S(1)}, f32[1,1,512,256]{3,2,1,0:T(8,128)S(1)}, u32[]{:S(2)}, u32[]{:S(2)}) collective-permute-start(f32[1,1,512,256]{3,2,1,0:T(8,128)S(1)} %get-tuple-element.51), channel_id=1, source_target_pairs={{0,1},{1,2},{2,3},{3,4},{4,5},{5,6},{6,7},{8,9},{9,10},{10,11},{11... | collective-permute-start | bytes 1572872 | tf_op jit(solution)/shard_map/ppermute | solution.py:36
  105.0 65.9 %collective-permute-start.16 = (f32[1,1,512,256]{3,2,1,0:T(8,128)}, f32[1,1,512,256]{3,2,1,0:T(8,128)}, u32[]{:S(2)}, u32[]{:S(2)}) collective-permute-start(f32[1,1,512,256]{3,2,1,0:T(8,128)} %get-tuple-element.50), channel_id=1, source_target_pairs={{1,0},{2,1},{3,2},{4,3},{5,4},{6,5},{7,6},{9,8},{10,9},{11,10},{12... | collective-permute-start | bytes 1572872 | tf_op jit(solution)/shard_map/ppermute | solution.py:37
  106.3 64.6 %collective-permute-start.17 = (f32[1,1,512,256]{3,2,1,0:T(8,128)}, f32[1,1,512,256]{3,2,1,0:T(8,128)}, u32[]{:S(2)}, u32[]{:S(2)}) collective-permute-start(f32[1,1,512,256]{3,2,1,0:T(8,128)} %get-tuple-element.50), channel_id=1, source_target_pairs={{0,1},{1,2},{2,3},{3,4},{4,5},{5,6},{6,7},{8,9},{9,10},{10,11},{11... | collective-permute-start | bytes 1572872 | tf_op jit(solution)/shard_map/ppermute | solution.py:36
  164.6 13.4 %collective-permute-start.6 = (f32[1,1,512,256]{3,2,1,0:T(8,128)S(1)}, f32[1,1,512,256]{3,2,1,0:T(8,128)S(1)}, u32[]{:S(2)}, u32[]{:S(2)}) collective-permute-start(f32[1,1,512,256]{3,2,1,0:T(8,128)S(1)} %multiply_subtract_fusion.4), channel_id=1, source_target_pairs={{1,0},{2,1},{3,2},{4,3},{5,4},{6,5},{7,6},{9,8},{10,9},{11,10},{12... | collective-permute-start | bytes 1572872 | tf_op jit(solution)/shard_map/ppermute | solution.py:37
  165.9 19.8 %collective-permute-start.7 = (f32[1,1,512,256]{3,2,1,0:T(8,128)S(1)}, f32[1,1,512,256]{3,2,1,0:T(8,128)S(1)}, u32[]{:S(2)}, u32[]{:S(2)}) collective-permute-start(f32[1,1,512,256]{3,2,1,0:T(8,128)S(1)} %multiply_subtract_fusion.4), channel_id=1, source_target_pairs={{0,1},{1,2},{2,3},{3,4},{4,5},{5,6},{6,7},{8,9},{9,10},{10,11},{11... | collective-permute-start | bytes 1572872 | tf_op jit(solution)/shard_map/ppermute | solution.py:36
  215.6 11.1 %collective-permute-start.8 = (f32[1,1,512,256]{3,2,1,0:T(8,128)S(1)}, f32[1,1,512,256]{3,2,1,0:T(8,128)S(1)}, u32[]{:S(2)}, u32[]{:S(2)}) collective-permute-start(f32[1,1,512,256]{3,2,1,0:T(8,128)S(1)} %get-tuple-element.40), channel_id=1, source_target_pairs={{1,0},{2,1},{3,2},{4,3},{5,4},{6,5},{7,6},{9,8},{10,9},{11,10},{12... | collective-permute-start | bytes 1572872 | tf_op jit(solution)/shard_map/ppermute | solution.py:37
  216.8 18.7 %collective-permute-start.9 = (f32[1,1,512,256]{3,2,1,0:T(8,128)S(1)}, f32[1,1,512,256]{3,2,1,0:T(8,128)S(1)}, u32[]{:S(2)}, u32[]{:S(2)}) collective-permute-start(f32[1,1,512,256]{3,2,1,0:T(8,128)S(1)} %get-tuple-element.40), channel_id=1, source_target_pairs={{0,1},{1,2},{2,3},{3,4},{4,5},{5,6},{6,7},{8,9},{9,10},{10,11},{11... | collective-permute-start | bytes 1572872 | tf_op jit(solution)/shard_map/ppermute | solution.py:36
  260.4 11.7 %collective-permute-start.10 = (f32[1,1,512,256]{3,2,1,0:T(8,128)S(1)}, f32[1,1,512,256]{3,2,1,0:T(8,128)S(1)}, u32[]{:S(2)}, u32[]{:S(2)}) collective-permute-start(f32[1,1,512,256]{3,2,1,0:T(8,128)S(1)} %multiply_subtract_fusion.3), channel_id=1, source_target_pairs={{1,0},{2,1},{3,2},{4,3},{5,4},{6,5},{7,6},{9,8},{10,9},{11,10},{12... | collective-permute-start | bytes 1572872 | tf_op jit(solution)/shard_map/ppermute | solution.py:37
  261.7 19.3 %collective-permute-start.11 = (f32[1,1,512,256]{3,2,1,0:T(8,128)S(1)}, f32[1,1,512,256]{3,2,1,0:T(8,128)S(1)}, u32[]{:S(2)}, u32[]{:S(2)}) collective-permute-start(f32[1,1,512,256]{3,2,1,0:T(8,128)S(1)} %multiply_subtract_fusion.3), channel_id=1, source_target_pairs={{0,1},{1,2},{2,3},{3,4},{4,5},{5,6},{6,7},{8,9},{9,10},{10,11},{11... | collective-permute-start | bytes 1572872 | tf_op jit(solution)/shard_map/ppermute | solution.py:36
  309.6 12.0 %collective-permute-start.12 = (f32[1,1,512,256]{3,2,1,0:T(8,128)S(1)}, f32[1,1,512,256]{3,2,1,0:T(8,128)S(1)}, u32[]{:S(2)}, u32[]{:S(2)}) collective-permute-start(f32[1,1,512,256]{3,2,1,0:T(8,128)S(1)} %get-tuple-element.37), channel_id=1, source_target_pairs={{1,0},{2,1},{3,2},{4,3},{5,4},{6,5},{7,6},{9,8},{10,9},{11,10},{12... | collective-permute-start | bytes 1572872 | tf_op jit(solution)/shard_map/ppermute | solution.py:37
  310.9 19.9 %collective-permute-start.13 = (f32[1,1,512,256]{3,2,1,0:T(8,128)S(1)}, f32[1,1,512,256]{3,2,1,0:T(8,128)S(1)}, u32[]{:S(2)}, u32[]{:S(2)}) collective-permute-start(f32[1,1,512,256]{3,2,1,0:T(8,128)S(1)} %get-tuple-element.37), channel_id=1, source_target_pairs={{0,1},{1,2},{2,3},{3,4},{4,5},{5,6},{6,7},{8,9},{9,10},{10,11},{11... | collective-permute-start | bytes 1572872 | tf_op jit(solution)/shard_map/ppermute | solution.py:36
  357.4 44.0 %copy-start.23 = (f32[1,1,512,256]{3,2,1,0:T(8,128)}, f32[1,1,512,256]{3,2,1,0:T(8,128)S(1)}, u32[]{:S(2)}) copy-start(f32[1,1,512,256]{3,2,1,0:T(8,128)S(1)} %get-tuple-element.97) | copy-start | bytes 1572868
  357.7 16.7 %collective-permute-start.18 = (f32[1,1,512,256]{3,2,1,0:T(8,128)S(1)}, f32[1,1,512,256]{3,2,1,0:T(8,128)S(1)}, u32[]{:S(2)}, u32[]{:S(2)}) collective-permute-start(f32[1,1,512,256]{3,2,1,0:T(8,128)S(1)} %get-tuple-element.96), channel_id=1, source_target_pairs={{1,0},{2,1},{3,2},{4,3},{5,4},{6,5},{7,6},{9,8},{10,9},{11,10},{12... | collective-permute-start | bytes 1572872 | tf_op jit(solution)/shard_map/ppermute | solution.py:37
  359.0 31.2 %collective-permute-start.19 = (f32[1,1,512,256]{3,2,1,0:T(8,128)S(1)}, f32[1,1,512,256]{3,2,1,0:T(8,128)S(1)}, u32[]{:S(2)}, u32[]{:S(2)}) collective-permute-start(f32[1,1,512,256]{3,2,1,0:T(8,128)S(1)} %get-tuple-element.96), channel_id=1, source_target_pairs={{0,1},{1,2},{2,3},{3,4},{4,5},{5,6},{6,7},{8,9},{9,10},{10,11},{11... | collective-permute-start | bytes 1572872 | tf_op jit(solution)/shard_map/ppermute | solution.py:36
  363.8 27.7 %collective-permute-start.14 = (f32[1,1,512,256]{3,2,1,0:T(8,128)S(1)}, f32[1,1,512,256]{3,2,1,0:T(8,128)S(1)}, u32[]{:S(2)}, u32[]{:S(2)}) collective-permute-start(f32[1,1,512,256]{3,2,1,0:T(8,128)S(1)} %get-tuple-element.97), channel_id=1, source_target_pairs={{1,0},{2,1},{3,2},{4,3},{5,4},{6,5},{7,6},{9,8},{10,9},{11,10},{12... | collective-permute-start | bytes 1572872 | tf_op jit(solution)/shard_map/ppermute | solution.py:37
  365.1 36.3 %collective-permute-start.15 = (f32[1,1,512,256]{3,2,1,0:T(8,128)S(1)}, f32[1,1,512,256]{3,2,1,0:T(8,128)S(1)}, u32[]{:S(2)}, u32[]{:S(2)}) collective-permute-start(f32[1,1,512,256]{3,2,1,0:T(8,128)S(1)} %get-tuple-element.97), channel_id=1, source_target_pairs={{0,1},{1,2},{2,3},{3,4},{4,5},{5,6},{6,7},{8,9},{9,10},{10,11},{11... | collective-permute-start | bytes 1572872 | tf_op jit(solution)/shard_map/ppermute | solution.py:36
  434.9 16.3 %collective-permute-start.20 = (f32[2,1,512,256]{3,2,1,0:T(8,128)}, f32[2,1,512,256]{3,2,1,0:T(8,128)S(1)}, u32[]{:S(2)}, u32[]{:S(2)}) collective-permute-start(f32[2,1,512,256]{3,2,1,0:T(8,128)} %pad_maximum_fusion), channel_id=1, source_target_pairs={{0,8},{8,16},{16,24},{1,9},{9,17},{17,25},{2,10},{10,18},{18,26},{... | collective-permute-start | bytes 3145736 | tf_op jit(solution)/shard_map/ppermute | solution.py:45
  (33 other events, 438.5 us)
where the time goes:
time: 454 us; the launch traced here: 452 us
  waiting for transfers between devices  196 us (43%)
  blocking collectives  125 us (28%)
  starting transfers between devices  63.3 us (14%)
  other arithmetic  31.9 us (7%)
  between operations  24.4 us (5%)
  local copies, waits for them, and re-layouts  11.5 us (3%)
    ppermute x10, waiting for transfers between devices, padded_2(): before = lax.ppermute(last, axis, up)  126 us
    psum x6, blocking collectives, paired(): lax.psum((inner(residual, residual), inner(residual, image)), 'space')  125 us
    ppermute x10, waiting for transfers between devices, padded_2(): after = lax.ppermute(leading, axis, down)  57.1 us
    ppermute x10, starting transfers between devices, padded_2(): before = lax.ppermute(last, axis, up)  48.4 us
    reduce_sum x8, other arithmetic, inner(): return jnp.sum(left * right, axis=(1, 2, 3))  14.1 us
    ppermute x1, waiting for transfers between devices, from_behind(): return lax.ppermute(block, axis, route)  13.1 us
    ppermute x10, starting transfers between devices, padded_2(): after = lax.ppermute(leading, axis, down)  13 us
  transfers between devices with their start and end apart: 21, of which 15 were waited for; matrix products, arithmetic and copies ran while one was open for 4% of the time, Pallas kernels for 0%

commit v1 on v0

v1 whole, which is shorter than its diff:
```python
import math

import jax
import jax.numpy as jnp
from jax import lax
from jax.experimental import pallas as pl
from jax.experimental.pallas import tpu as pltpu
from jax.sharding import PartitionSpec as P

AXES = ("tm", "space")
STEP = 2.0
ROOT_SIX = math.sqrt(6.0)
NODE_TIMES = [(4.0 - ROOT_SIX) / 10.0, (4.0 + ROOT_SIX) / 10.0, 1.0]
COLLOC = [
    [
        (88.0 - 7.0 * ROOT_SIX) / 360.0,
        (296.0 - 169.0 * ROOT_SIX) / 1800.0,
        (-2.0 + 3.0 * ROOT_SIX) / 225.0,
    ],
    [
        (296.0 + 169.0 * ROOT_SIX) / 1800.0,
        (88.0 + 7.0 * ROOT_SIX) / 360.0,
        (-2.0 - 3.0 * ROOT_SIX) / 225.0,
    ],
    [(16.0 - ROOT_SIX) / 36.0, (16.0 + ROOT_SIX) / 36.0, 1.0 / 9.0],
]
ROWS = 16
KINDS = 16
LANES = 128


def sweep_weight(row, column):
    below = COLLOC[row - 1][column] if row > 0 else 0.0
    return COLLOC[row][column] - below


def node_width(row):
    below = NODE_TIMES[row - 1] if row > 0 else 0.0
    return NODE_TIMES[row] - below


class Places:
    def __init__(self, slices, planes):
        self.slices, self.planes = slices, planes
        self.crossed = slices % 2 == 0 and planes % 2 == 0

    def flat(self, t, s):
        return t * self.planes + s

    def device(self, t, p):
        if not self.crossed:
            return self.flat(t, p)
        return self.flat(2 * (t // 2) + p % 2, 2 * (p // 2) + t % 2)

    def every(self):
        return [(t, p) for t in range(self.slices) for p in range(self.planes)]

    def swap(self):
        return [(self.flat(t, p), self.device(t, p)) for t, p in self.every()]

    def to_next(self):
        return [(self.device(t, p), self.flat(t + 1, p)) for t, p in self.every() if t + 1 < self.slices]

    def pairs(self, odd):
        partner = lambda p: p + 1 if p % 2 == odd else p - 1
        return [
            (self.device(t, p), self.device(t, partner(p)))
            for t, p in self.every()
            if 0 <= partner(p) < self.planes
        ]

    def rounds(self):
        left, stride, found = self.planes, 1, []
        while left > 1:
            factor = next(f for f in range(2, left + 1) if left % f == 0)
            turns = []
            for turn in range(1, factor):
                moved = lambda p: p + (((p // stride + turn) % factor) - (p // stride) % factor) * stride
                turns.append([(self.device(t, p), self.device(t, moved(p))) for t, p in self.every()])
            found.append(turns)
            left, stride = left // factor, stride * factor
        return found


def own_plane(places):
    t, s = lax.axis_index("tm"), lax.axis_index("space")
    return 2 * (s // 2) + t % 2 if places.crossed else s


def move(value, perm):
    return lax.ppermute(value, AXES, perm)


def row_after(ref, lead, start, count):
    total = ref.shape[-2]
    if start + count + 1 <= total:
        return ref[(*lead, slice(start + 1, start + count + 1), slice(None))]
    return pltpu.roll(ref[(*lead, slice(start, start + count), slice(None))], count - 1, 0)


def row_before(ref, lead, start, count):
    if start > 0:
        return ref[(*lead, slice(start - 1, start + count - 1), slice(None))]
    return pltpu.roll(ref[(*lead, slice(0, count), slice(None))], 1, 0)


def heat_rows(own, lead, beside, faces, start, count):
    rows = slice(start, start + count)
    here = own[(*lead, rows, slice(None))]
    width = here.shape[-1]
    face_x = faces[3, rows, :]
    result = faces[0, rows, :] * beside[0] + faces[1, rows, :] * beside[1]
    result += faces[2, rows, :] * row_after(own, lead, start, count)
    lower = row_before(faces, (2,), start, count) * row_before(own, lead, start, count)
    if start == 0:
        lower = jnp.where(lax.broadcasted_iota(jnp.int32, lower.shape, 0) == 0, 0.0, lower)
    result += lower
    result += face_x * pltpu.roll(here, width - 1, 1) + pltpu.roll(face_x * here, 1, 1)
    return result - faces[4, rows, :] * here, here


def chunks(ref):
    total = ref.shape[-2]
    return [(start, min(ROWS, total - start)) for start in range(0, total, ROWS)]


def faces_kernel(kappa, kappa_a, kappa_b, faces):
    length, width = kappa.shape
    for start, count in chunks(kappa):
        rows = slice(start, start + count)
        here = kappa[rows, :]
        face_a = 0.5 * (here + kappa_a[rows, :])
        face_b = 0.5 * (here + kappa_b[rows, :])
        after = row_after(kappa, (), start, count)
        before = row_before(kappa, (), start, count)
        row = lax.broadcasted_iota(jnp.int32, here.shape, 0) + start
        column = lax.broadcasted_iota(jnp.int32, here.shape, 1)
        after = jnp.where(row == length - 1, 0.0, after)
        before = jnp.where(row == 0, 0.0, before)
        right = jnp.where(column == width - 1, 0.0, pltpu.roll(here, width - 1, 1))
        left = jnp.where(column == 0, 0.0, pltpu.roll(here, 1, 1))
        face_y = 0.5 * (here + after)
        face_x = 0.5 * (here + right)
        faces[0, rows, :] = face_a
        faces[1, rows, :] = face_b
        faces[2, rows, :] = jnp.where(row == length - 1, 0.0, face_y)
        faces[3, rows, :] = jnp.where(column == width - 1, 0.0, face_x)
        faces[4, rows, :] = face_a + face_b + face_y + face_x + 0.5 * (here + before) + 0.5 * (here + left)


def increments_kernel(begin, *refs):
    nodes, beside_a, beside_b, faces, outs = refs[:3], refs[3:6], refs[6:9], refs[9], refs[10:]
    for start, count in chunks(begin):
        rows = slice(start, start + count)
        images, values = [], [begin[rows, :]]
        for column in range(3):
            image, here = heat_rows(
                nodes[column], (), (beside_a[column][rows, :], beside_b[column][rows, :]), faces, start, count
            )
            images.append(image)
            values.append(here)
        for row in range(3):
            change = values[row] - values[row + 1]
            for column in range(3):
                change += (STEP * sweep_weight(row, column)) * images[column]
            outs[row][rows, :] = change


def apply_kernel(width, count_in, *refs):
    own, beside_a, beside_b = refs[:count_in], refs[count_in : 2 * count_in], refs[2 * count_in : 3 * count_in]
    faces, out = refs[3 * count_in], refs[3 * count_in + 1 :]
    field = own[0]
    if count_in > 1:
        field = out[1]
        for start, count in chunks(field):
            rows = slice(start, start + count)
            field[rows, :] = sum(ref[rows, :] for ref in own)
    for start, count in chunks(field):
        rows = slice(start, start + count)
        beside = (sum(ref[rows, :] for ref in beside_a), sum(ref[rows, :] for ref in beside_b))
        image, here = heat_rows(field, (), beside, faces, start, count)
        out[0][rows, :] = here - width * image


def folded(value):
    return jnp.sum(value.reshape(value.shape[0] // 8, 8, value.shape[1]), axis=0)


def whole_sum(value):
    return jnp.sum(jnp.sum(value, axis=0, keepdims=True), axis=1, keepdims=True)


def moments_kernel(width, place, residual, image, image_a, image_b, faces, out):
    zero = jnp.zeros((8, residual.shape[1]), jnp.float32)
    rr, rq, qq = zero, zero, zero
    for start, count in chunks(residual):
        rows = slice(start, start + count)
        r, q = residual[rows, :], image[rows, :]
        rr, rq, qq = rr + folded(r * r), rq + folded(r * q), qq + folded(q * q)
    rr, rq, qq = whole_sum(rr), whole_sum(rq), whole_sum(qq)
    centre = jnp.where(qq > 0.0, rq / jnp.where(qq > 0.0, qq, 1.0), 0.0)
    sums = [zero] * 6
    for start, count in chunks(residual):
        rows = slice(start, start + count)
        heat, q = heat_rows(image, (), (image_a[rows, :], image_b[rows, :]), faces, start, count)
        aq = q - width * heat
        w = residual[rows, :] - centre * q
        aw = q - centre * aq
        terms = (w * w, w * q, w * aw, w * aq, q * aw, q * aq)
        sums = [total + folded(term) for total, term in zip(sums, terms)]
    values = [rr, rq, qq, centre] + [whole_sum(total) for total in sums]
    kind = lax.broadcasted_iota(jnp.int32, out.shape, 0)
    lane = lax.broadcasted_iota(jnp.int32, out.shape, 1)
    message = jnp.zeros(out.shape, jnp.float32)
    for index, value in enumerate(values):
        message = jnp.where(kind == index, value, message)
    out[...] = jnp.where(lane == place[0], message, 0.0)


def step_weights(gathered):
    row = lambda index: gathered[index : index + 1, :]
    total = lambda value: jnp.sum(value, axis=1, keepdims=True)
    rr, rq = total(row(0)), total(row(1))
    step = rr / rq
    away = step - row(3)
    rr_next = total(row(4) - 2.0 * away * row(5) + away * away * row(2))
    energy = total(row(6) - away * (row(7) + row(8)) + away * away * row(9))
    momentum = rr_next / rr
    step_next = rr_next / (energy - momentum * rr_next / step)
    return step + step_next * (1.0 + momentum), -step_next * step


def advance_kernel(width, keep, gathered, guess, *refs):
    grown, residual, image, faces = refs[0:3], refs[3:6], refs[6:9], refs[9]
    result, product, following = refs[10], refs[11], refs[12:]
    first, second = step_weights(gathered[...])
    for start, count in chunks(guess):
        rows = slice(start, start + count)
        change = first * residual[0][rows, :] + second * image[0][rows, :]
        result[rows, :] = guess[rows, :] + change
        following[0][rows, :] = grown[0][rows, :] + change
    for start, count in chunks(guess):
        rows = slice(start, start + count)
        beside = []
        for side in (1, 2):
            value = grown[side][rows, :] + first * residual[side][rows, :] + second * image[side][rows, :]
            if keep:
                following[side][rows, :] = value
            beside.append(value)
        heat, here = heat_rows(following[0], (), beside, faces, start, count)
        product[rows, :] = here - width * heat


def finish_kernel(gathered, guess, residual, image, out):
    first, second = step_weights(gathered[...])
    for start, count in chunks(guess):
        rows = slice(start, start + count)
        out[rows, :] = guess[rows, :] + first * residual[rows, :] + second * image[rows, :]


VMEM = pl.BlockSpec(memory_space=pltpu.VMEM)
SMEM = pl.BlockSpec(memory_space=pltpu.SMEM)


def call(kernel, shapes, *args, scalars=0):
    single = not isinstance(shapes, list)
    outs = [jax.ShapeDtypeStruct(shape, jnp.float32) for shape in ([shapes] if single else shapes)]
    found = pl.pallas_call(
        kernel,
        out_shape=outs,
        in_specs=[SMEM] * scalars + [VMEM] * (len(args) - scalars),
        out_specs=[VMEM] * len(outs),
    )(*args)
    return found[0] if single else found


def on_device(places, start_value, old_nodes, diffusivity):
    plane = diffusivity.shape[1:]
    swap, near, far = places.swap(), places.pairs(0), places.pairs(1)
    place = own_plane(places).astype(jnp.int32).reshape(1)

    def sides(value):
        return move(value, far), move(value, near)

    def gather(message):
        for turns in places.rounds():
            message = sum([move(message, perm) for perm in turns], message)
        return message

    def moments(width, residual, image, beside, faces):
        lanes = LANES * (-(-places.planes // LANES))
        return call(
            lambda *refs: moments_kernel(width, *refs),
            (KINDS, lanes),
            place,
            residual,
            image,
            *beside,
            faces,
            scalars=1,
        )

    kappa = move(diffusivity[0], swap)
    nodes = [move(old_nodes[0, column, 0], swap) for column in range(3)]
    begin = move(start_value[0, 0], swap)
    kappa_sides = sides(kappa)
    node_sides = [sides(node) for node in nodes]
    faces = call(faces_kernel, (5, *plane), kappa, *kappa_sides)
    grown = call(
        increments_kernel,
        [plane] * 3,
        begin,
        *nodes,
        *[pair[0] for pair in node_sides],
        *[pair[1] for pair in node_sides],
        faces,
    )
    grown_sides = [sides(value) for value in grown]
    trio = [(grown[m], *grown_sides[m]) for m in range(3)]
    widths = [STEP * node_width(row) for row in range(3)]

    residual = trio[0]
    image = call(lambda *refs: apply_kernel(widths[0], 1, *refs), plane, *residual, faces)
    image_trio = (image, *sides(image))
    fresh = []
    for row in range(2):
        gathered = gather(moments(widths[row], residual[0], image, image_trio[1:], faces))
        keep = row == 0
        found = call(
            lambda *refs: advance_kernel(widths[row + 1], keep, *refs),
            [plane] * (5 if keep else 3),
            gathered,
            nodes[row],
            *trio[row + 1],
            *residual,
            *image_trio,
            faces,
        )
        fresh.append(found[0])
        image, residual = found[1], found[2:]
        image_trio = (image, *sides(image))
    gathered = gather(moments(widths[2], residual[0], image, image_trio[1:], faces))
    fresh.append(call(finish_kernel, plane, gathered, nodes[2], residual[0], image))

    coarse_image, coarse = call(
        lambda *refs: apply_kernel(STEP, 3, *refs),
        [plane] * 2,
        *grown,
        *[pair[0] for pair in grown_sides],
        *[pair[1] for pair in grown_sides],
        faces,
    )
    coarse_gathered = gather(moments(STEP, coarse, coarse_image, sides(coarse_image), faces))
    coarse_end = call(finish_kernel, plane, coarse_gathered, nodes[2], coarse, coarse_image)

    next_coarse = move(coarse_end, places.to_next())
    next_start = move(fresh[2], places.to_next())
    fine_nodes = jnp.stack([move(value, swap) for value in fresh])[None, :, None]
    first_slice = lax.axis_index("tm") == 0
    next_start = jnp.where(first_slice, start_value, next_start[None, None])
    next_coarse = jnp.where(first_slice, start_value, next_coarse[None, None])
    return fine_nodes, next_start, next_coarse


def solution(mesh):
    places = Places(mesh.shape["tm"], mesh.shape["space"])
    return jax.shard_map(
        lambda *args: on_device(places, *args),
        mesh=mesh,
        in_specs=(
            P("tm", "space", None, None),
            P("tm", None, "space", None, None),
            P("space", None, None),
        ),
        out_specs=(
            P("tm", None, "space", None, None),
            P("tm", "space", None, None),
            P("tm", "space", None, None),
        ),
        check_vma=False,
    )
```

time: 454 us -> 222 us (0.49)
  waiting for transfers between devices: 196 us -> 43.4 us
  blocking collectives: 125 us -> 0 us
  Pallas kernels: 0 us -> 49 us
  starting transfers between devices: 63.3 us -> 110 us
  other arithmetic: 31.9 us -> 7.51 us
  between operations: 24.4 us -> 1.08 us
    ppermute x21 -> x44, waiting for transfers between devices: 196 us -> 43.4 us  [move(): return lax.ppermute(value, AXES, perm)]
    psum x6 -> x0, blocking collectives: 125 us -> none  [paired(): lax.psum((inner(residual, residual), inner(residual, image)), 'space')]
    pallas_call x0 -> x12, Pallas kernels: none -> 49 us  [call(): pl.pallas_call(kernel, out_shape=outs, in_specs=[SMEM] * scalars + [VMEM]...]
    ppermute x21 -> x44, starting transfers between devices: 63.3 us -> 110 us  [move(): return lax.ppermute(value, AXES, perm)]
    reduce_sum x8 -> x0, other arithmetic: 14.1 us -> none  [inner(): return jnp.sum(left * right, axis=(1, 2, 3))]
    slice x20 -> x0, local copies, waits for them, and re-layouts: 8.88 us -> none  [the longest x18 7.4 us: neighbour(): lax.slice_in_dim(field, 1, length, axis=dim)]
    unnamed x72 -> x52, local copies, waits for them, and re-layouts: 2.61 us -> 8.84 us
    sub x4 -> x0, other arithmetic: 5.55 us -> none  [the longest x3 4.19 us: solve(): residual = residual - widen(step_size) * along_image]
  transfers between devices with their start and end apart: 21 -> 44, of which waited for: 15 -> 14; matrix products, arithmetic and copies ran while one was open for 4% -> 4% of each run, Pallas kernels for 0% -> 13%
where the time goes in v1:
time: 222 us; the launch traced here: 221 us
  starting transfers between devices  110 us (50%)
  Pallas kernels  49 us (22%)
  waiting for transfers between devices  43.4 us (20%)
  local copies, waits for them, and re-layouts  10.3 us (5%)
  other arithmetic  7.51 us (3%)
    ppermute x44, starting transfers between devices, move(): return lax.ppermute(value, AXES, perm)  110 us
    pallas_call x12, Pallas kernels, call(): pl.pallas_call(kernel, out_shape=outs, in_specs=[SMEM] * scalars + [VMEM]...  49 us
    ppermute x44, waiting for transfers between devices, move(): return lax.ppermute(value, AXES, perm)  43.4 us
    unnamed x52, local copies, waits for them, and re-layouts  8.84 us
    add x12, other arithmetic, gather(): message = sum([move(message, perm) for perm in turns], message)  5.2 us
  transfers between devices with their start and end apart: 44, of which 14 were waited for; matrix products, arithmetic and copies ran while one was open for 4% of the time, Pallas kernels for 13%

profile of v1, /device:TPU:2, one launch (start us, length us, event | category | flops | bytes accessed | tf_op | source)
XLA Modules:
  0.0 221.1 jit_solution(14396975689287738817)
XLA Ops:
  7.6 9.3 %collective-permute-start.12 = (f32[512,256]{1,0:T(8,128)S(1)}, f32[512,256]{1,0:T(8,128)S(1)}, u32[]{:S(2)}, u32[]{:S(2)}) collective-permute-start(f32[512,256]{1,0:T(8,128)S(1)} %collective-permute-done.10.kappa), channel_id=1, source_target_pairs={{0,8},{8,0},{2,10},{10,2},{4,12},{12,4},{6,14},{14,6},{1,9},{9,1},... | collective-permute-start | bytes 1572872 | tf_op jit(solution)/shard_map/ppermute | solution.py:91
  17.6 4.9 %collective-permute-start.9 = (f32[512,256]{1,0:T(8,128)S(1)}, f32[512,256]{1,0:T(8,128)S(1)}, u32[]{:S(2)}, u32[]{:S(2)}) collective-permute-start(f32[512,256]{1,0:T(8,128)S(1)} %collective-permute-done.3.refs_2_.guess), channel_id=1, source_target_pairs={{0,8},{8,0},{2,10},{10,2},{4,12},{12,4},{6,14},{14,6},{1,9},{9,1},... | collective-permute-start | bytes 1572872 | tf_op jit(solution)/shard_map/ppermute | solution.py:91
  23.9 9.8 %collective-permute-start.7 = (f32[512,256]{1,0:T(8,128)S(1)}, f32[512,256]{1,0:T(8,128)}, u32[]{:S(2)}, u32[]{:S(2)}) collective-permute-start(f32[512,256]{1,0:T(8,128)S(1)} %collective-permute-done.1.refs_0_.refs_1_), channel_id=1, source_target_pairs={{0,8},{8,0},{2,10},{10,2},{4,12},{12,4},{6,14},{14,6},{1,9},{9,1},... | collective-permute-start | bytes 1572872 | tf_op jit(solution)/shard_map/ppermute | solution.py:91
  40.1 3.3 %shard_map.58.refs_9_.refs_3_.refs_5_.refs_11_ = f32[5,512,256]{2,1,0:T(8,128)} custom-call(f32[512,256]{1,0:T(8,128)} %copy-done.21, f32[512,256]{1,0:T(8,128)} %copy-done.23, f32[512,256]{1,0:T(8,128)} %copy-done.22), custom_call_target="tpu_custom_call" | custom-call | tf_op jit(solution)/shard_map/pallas_call | solution.py:268
  43.4 6.0 %shard_map.59 = (f32[512,256]{1,0:T(8,128)}, f32[512,256]{1,0:T(8,128)}, f32[512,256]{1,0:T(8,128)}) custom-call(f32[512,256]{1,0:T(8,128)} %copy-done.24, f32[512,256]{1,0:T(8,128)} %copy-done.14, f32[512,256]{1,0:T(8,128)} %copy-done.13, f32[512,256]{1,0:T(8,128)} %copy-done.2, f32[512,256]{1,0:T(8,128)} %collective-permute-done.4.refs_3_, ...), custom_call_target="tpu_custom_call" | custom-call | tf_op jit(solution)/shard_map/pallas_call | solution.py:268
  49.5 6.8 %collective-permute-start.14 = (f32[512,256]{1,0:T(8,128)}, f32[512,256]{1,0:T(8,128)S(1)}, u32[]{:S(2)}, u32[]{:S(2)}) collective-permute-start(f32[512,256]{1,0:T(8,128)} %get-tuple-element.16.refs_0_.refs_1_.refs_5_), channel_id=1, source_target_pairs={{0,8},{8,0},{2,10},{10,2},{4,12},{12,4},{6,14},{14,6},{1,9},{9,1},... | collective-permute-start | bytes 1572872 | tf_op jit(solution)/shard_map/ppermute | solution.py:91
  59.7 3.5 %shard_map.60.refs_2_.refs_8_ = f32[512,256]{1,0:T(8,128)} custom-call(f32[512,256]{1,0:T(8,128)} %get-tuple-element.16.refs_0_.refs_1_.refs_5_, f32[512,256]{1,0:T(8,128)} %copy-done.1, f32[512,256]{1,0:T(8,128)} %copy-done, f32[5,512,256]{2,1,0:T(8,128)} %shard_map.58.refs_9_.refs_3_.refs_5_.refs_11_), custom_call_target="tpu_custom_call" | custom-call | tf_op jit(solution)/shard_map/pallas_call | solution.py:268
  63.2 8.4 %collective-permute-start.16 = (f32[512,256]{1,0:T(8,128)}, f32[512,256]{1,0:T(8,128)S(1)}, u32[]{:S(2)}, u32[]{:S(2)}) collective-permute-start(f32[512,256]{1,0:T(8,128)} %shard_map.60.refs_2_.refs_8_), channel_id=1, source_target_pairs={{0,8},{8,0},{2,10},{10,2},{4,12},{12,4},{6,14},{14,6},{1,9},{9,1},... | collective-permute-start | bytes 1572872 | tf_op jit(solution)/shard_map/ppermute | solution.py:91
  72.3 3.3 %collective-permute-start.21 = (f32[512,256]{1,0:T(8,128)S(1)}, f32[512,256]{1,0:T(8,128)S(1)}, u32[]{:S(2)}, u32[]{:S(2)}) collective-permute-start(f32[512,256]{1,0:T(8,128)S(1)} %copy-done.3), channel_id=1, source_target_pairs={{0,8},{8,0},{2,10},{10,2},{4,12},{12,4},{6,14},{14,6},{1,9},{9,1},... | collective-permute-start | bytes 1572872 | tf_op jit(solution)/shard_map/ppermute | solution.py:91
  77.3 3.9 %shard_map.61 = f32[16,128]{1,0:T(8,128)} custom-call(s32[1]{0:T(128)} %bitcast.refs_0_, f32[512,256]{1,0:T(8,128)} %get-tuple-element.16.refs_0_.refs_1_.refs_5_, f32[512,256]{1,0:T(8,128)} %shard_map.60.refs_2_.refs_8_, f32[512,256]{1,0:T(8,128)} %copy-done.10, f32[512,256]{1,0:T(8,128)} %copy-done.9, f32[5,512,256]{2,1,0:T(8,128)} %shard_map.58.refs_9_.refs_3_.refs_5_.refs_11_), custom_call_target="tpu_custom_call" | custom-call | tf_op jit(solution)/shard_map/pallas_call | solution.py:268
  81.2 6.1 %collective-permute-start.17 = (f32[16,128]{1,0:T(8,128)}, f32[16,128]{1,0:T(8,128)S(1)}, u32[]{:S(2)}, u32[]{:S(2)}) collective-permute-start(f32[16,128]{1,0:T(8,128)} %shard_map.61), channel_id=1, source_target_pairs={{0,8},{8,0},{2,10},{10,2},{4,12},{12,4},{6,14},{14,6},{1,9},{9,1},... | collective-permute-start | bytes 24584 | tf_op jit(solution)/shard_map/ppermute | solution.py:91
  99.7 5.7 %shard_map.62 = (f32[512,256]{1,0:T(8,128)}, f32[512,256]{1,0:T(8,128)}, f32[512,256]{1,0:T(8,128)}, f32[512,256]{1,0:T(8,128)}, f32[512,256]{1,0:T(8,128)}) custom-call(f32[16,128]{1,0:T(8,128)} %add.48.refs_0_, f32[512,256]{1,0:T(8,128)} %copy-done.14, f32[512,256]{1,0:T(8,128)} %get-tuple-element.17.refs_2_.refs_1_, f32[512,256]{1,0:T(8,128)} %copy-done.6, ...), custom_call_target="tpu_custom_call" | custom-call | tf_op jit(solution)/shard_map/pallas_call | solution.py:268
  106.1 3.3 %collective-permute-start.29 = (f32[512,256]{1,0:T(8,128)S(1)}, f32[512,256]{1,0:T(8,128)S(1)}, u32[]{:S(2)}, u32[]{:S(2)}) collective-permute-start(f32[512,256]{1,0:T(8,128)S(1)} %copy-done.4), channel_id=1, source_target_pairs={{0,8},{8,0},{2,10},{10,2},{4,12},{12,4},{6,14},{14,6},{1,9},{9,1},... | collective-permute-start | bytes 1572872 | tf_op jit(solution)/shard_map/ppermute | solution.py:91
  111.0 3.9 %shard_map.63 = f32[16,128]{1,0:T(8,128)} custom-call(s32[1]{0:T(128)} %bitcast.refs_0_, f32[512,256]{1,0:T(8,128)} %get-tuple-element.19.refs_1_.refs_5_, f32[512,256]{1,0:T(8,128)} %get-tuple-element.20.refs_2_.refs_8_, f32[512,256]{1,0:T(8,128)} %copy-done.12, f32[512,256]{1,0:T(8,128)} %copy-done.11, ...), custom_call_target="tpu_custom_call" | custom-call | tf_op jit(solution)/shard_map/pallas_call | solution.py:268
  114.9 6.3 %collective-permute-start.25 = (f32[16,128]{1,0:T(8,128)}, f32[16,128]{1,0:T(8,128)S(1)}, u32[]{:S(2)}, u32[]{:S(2)}) collective-permute-start(f32[16,128]{1,0:T(8,128)} %shard_map.63), channel_id=1, source_target_pairs={{0,8},{8,0},{2,10},{10,2},{4,12},{12,4},{6,14},{14,6},{1,9},{9,1},... | collective-permute-start | bytes 24584 | tf_op jit(solution)/shard_map/ppermute | solution.py:91
  133.1 5.3 %shard_map.64 = (f32[512,256]{1,0:T(8,128)}, f32[512,256]{1,0:T(8,128)}, f32[512,256]{1,0:T(8,128)}) custom-call(f32[16,128]{1,0:T(8,128)} %add.51.refs_0_, f32[512,256]{1,0:T(8,128)} %copy-done.13, f32[512,256]{1,0:T(8,128)} %get-tuple-element.21.refs_2_, f32[512,256]{1,0:T(8,128)} %copy-done.8, f32[512,256]{1,0:T(8,128)} %copy-done.7, ...), custom_call_target="tpu_custom_call" | custom-call | tf_op jit(solution)/shard_map/pallas_call | solution.py:268
  139.1 4.6 %shard_map.67 = (f32[512,256]{1,0:T(8,128)}, f32[512,256]{1,0:T(8,128)}) custom-call(f32[512,256]{1,0:T(8,128)} %get-tuple-element.16.refs_0_.refs_1_.refs_5_, f32[512,256]{1,0:T(8,128)} %get-tuple-element.17.refs_2_.refs_1_, f32[512,256]{1,0:T(8,128)} %get-tuple-element.21.refs_2_, f32[512,256]{1,0:T(8,128)} %copy-done.1, f32[512,256]{1,0:T(8,128)} %copy-done.6, ...), custom_call_target="tpu_custom_call" | custom-call | tf_op jit(solution)/shard_map/pallas_call | solution.py:268
  148.5 3.9 %shard_map.65 = f32[16,128]{1,0:T(8,128)} custom-call(s32[1]{0:T(128)} %bitcast.refs_0_, f32[512,256]{1,0:T(8,128)} %get-tuple-element.25.refs_1_.residual, f32[512,256]{1,0:T(8,128)} %get-tuple-element.26.refs_2_.image, f32[512,256]{1,0:T(8,128)} %copy-done.18, f32[512,256]{1,0:T(8,128)} %copy-done.17, f32[5,512,256]{2,1,0:T(8,128)} %shard_map.58.refs_9_.refs_3_.refs_5_.refs_11_), custom_call_target="tpu_custom_call" | custom-call | tf_op jit(solution)/shard_map/pallas_call | solution.py:268
  171.8 3.9 %shard_map.68 = f32[16,128]{1,0:T(8,128)} custom-call(s32[1]{0:T(128)} %bitcast.refs_0_, f32[512,256]{1,0:T(8,128)} %get-tuple-element.27.refs_1_.residual, f32[512,256]{1,0:T(8,128)} %get-tuple-element.28.refs_2_.image, f32[512,256]{1,0:T(8,128)} %copy-done.16, f32[512,256]{1,0:T(8,128)} %copy-done.15, f32[5,512,256]{2,1,0:T(8,128)} %shard_map.58.refs_9_.refs_3_.refs_5_.refs_11_), custom_call_target="tpu_custom_call" | custom-call | tf_op jit(solution)/shard_map/pallas_call | solution.py:268
  175.7 4.0 %collective-permute-start.40 = (f32[16,128]{1,0:T(8,128)}, f32[16,128]{1,0:T(8,128)S(1)}, u32[]{:S(2)}, u32[]{:S(2)}) collective-permute-start(f32[16,128]{1,0:T(8,128)} %shard_map.68), channel_id=1, source_target_pairs={{0,8},{8,0},{2,10},{10,2},{4,12},{12,4},{6,14},{14,6},{1,9},{9,1},... | collective-permute-start | bytes 24584 | tf_op jit(solution)/shard_map/ppermute | solution.py:91
  181.8 3.3 %collective-permute-done.41 = f32[16,128]{1,0:T(8,128)S(1)} collective-permute-done((f32[16,128]{1,0:T(8,128)S(1)}, f32[16,128]{1,0:T(8,128)S(1)}, u32[]{:S(2)}, u32[]{:S(2)}) %collective-permute-start.41) | collective-permute-done | bytes 8224 | tf_op jit(solution)/shard_map/ppermute | solution.py:91
  186.1 3.5 %collective-permute-done.42 = f32[16,128]{1,0:T(8,128)S(1)} collective-permute-done((f32[16,128]{1,0:T(8,128)S(1)}, f32[16,128]{1,0:T(8,128)S(1)}, u32[]{:S(2)}, u32[]{:S(2)}) %collective-permute-start.42) | collective-permute-done | bytes 8224 | tf_op jit(solution)/shard_map/ppermute | solution.py:91
  197.9 12.6 %collective-permute-done.43 = f32[512,256]{1,0:T(8,128)S(1)} collective-permute-done((f32[512,256]{1,0:T(8,128)}, f32[512,256]{1,0:T(8,128)S(1)}, u32[]{:S(2)}, u32[]{:S(2)}) %collective-permute-start.43) | collective-permute-done | bytes 524320 | tf_op jit(solution)/shard_map/ppermute | solution.py:91
  210.6 9.4 %collective-permute-done.37 = f32[512,256]{1,0:T(8,128)S(1)} collective-permute-done((f32[512,256]{1,0:T(8,128)S(1)}, f32[512,256]{1,0:T(8,128)S(1)}, u32[]{:S(2)}, u32[]{:S(2)}) %collective-permute-start.37) | collective-permute-done | bytes 524320 | tf_op jit(solution)/shard_map/ppermute | solution.py:91
  (143 shorter events, 85.0 us)
Async XLA Ops:
  2.3 14.6 %collective-permute-start = (f32[512,256]{1,0:T(8,128)}, f32[512,256]{1,0:T(8,128)S(1)}, u32[]{:S(2)}, u32[]{:S(2)}) collective-permute-start(f32[512,256]{1,0:T(8,128)} %bitcast.20), channel_id=1, source_target_pairs={{0,0},{1,8},{2,2},{3,10},{4,4},{5,12},{6,6},{7,14},{8,1},{9,9},{10... | collective-permute-start | bytes 1572872 | tf_op jit(solution)/shard_map/ppermute | solution.py:91
  5.5 12.1 %collective-permute-start.3 = (f32[512,256]{1,0:T(8,128)S(1)}, f32[512,256]{1,0:T(8,128)S(1)}, u32[]{:S(2)}, u32[]{:S(2)}) collective-permute-start(f32[512,256]{1,0:T(8,128)S(1)} %get-tuple-element.32), channel_id=1, source_target_pairs={{0,0},{1,8},{2,2},{3,10},{4,4},{5,12},{6,6},{7,14},{8,1},{9,9},{10... | collective-permute-start | bytes 1572872 | tf_op jit(solution)/shard_map/ppermute | solution.py:91
  6.2 16.3 %collective-permute-start.1 = (f32[512,256]{1,0:T(8,128)S(1)}, f32[512,256]{1,0:T(8,128)S(1)}, u32[]{:S(2)}, u32[]{:S(2)}) collective-permute-start(f32[512,256]{1,0:T(8,128)S(1)} %get-tuple-element.33), channel_id=1, source_target_pairs={{0,0},{1,8},{2,2},{3,10},{4,4},{5,12},{6,6},{7,14},{8,1},{9,9},{10... | collective-permute-start | bytes 1572872 | tf_op jit(solution)/shard_map/ppermute | solution.py:91
  6.9 17.0 %collective-permute-start.2 = (f32[512,256]{1,0:T(8,128)S(1)}, f32[512,256]{1,0:T(8,128)S(1)}, u32[]{:S(2)}, u32[]{:S(2)}) collective-permute-start(f32[512,256]{1,0:T(8,128)S(1)} %get-tuple-element.34), channel_id=1, source_target_pairs={{0,0},{1,8},{2,2},{3,10},{4,4},{5,12},{6,6},{7,14},{8,1},{9,9},{10... | collective-permute-start | bytes 1572872 | tf_op jit(solution)/shard_map/ppermute | solution.py:91
  7.6 26.1 %collective-permute-start.12 = (f32[512,256]{1,0:T(8,128)S(1)}, f32[512,256]{1,0:T(8,128)S(1)}, u32[]{:S(2)}, u32[]{:S(2)}) collective-permute-start(f32[512,256]{1,0:T(8,128)S(1)} %collective-permute-done.10.kappa), channel_id=1, source_target_pairs={{0,8},{8,0},{2,10},{10,2},{4,12},{12,4},{6,14},{14,6},{1,9},{9,1},... | collective-permute-start | bytes 1572872 | tf_op jit(solution)/shard_map/ppermute | solution.py:91
  16.9 18.3 %collective-permute-start.11 = (f32[512,256]{1,0:T(8,128)S(1)}, f32[512,256]{1,0:T(8,128)S(1)}, u32[]{:S(2)}, u32[]{:S(2)}) collective-permute-start(f32[512,256]{1,0:T(8,128)S(1)} %collective-permute-done.10.kappa), channel_id=1, source_target_pairs={{8,2},{2,8},{10,4},{4,10},{12,6},{6,12},{9,3},{3,9},{11,5},{5,11},... | collective-permute-start | bytes 1572872 | tf_op jit(solution)/shard_map/ppermute | solution.py:91
  17.6 20.2 %collective-permute-start.9 = (f32[512,256]{1,0:T(8,128)S(1)}, f32[512,256]{1,0:T(8,128)S(1)}, u32[]{:S(2)}, u32[]{:S(2)}) collective-permute-start(f32[512,256]{1,0:T(8,128)S(1)} %collective-permute-done.3.refs_2_.guess), channel_id=1, source_target_pairs={{0,8},{8,0},{2,10},{10,2},{4,12},{12,4},{6,14},{14,6},{1,9},{9,1},... | collective-permute-start | bytes 1572872 | tf_op jit(solution)/shard_map/ppermute | solution.py:91
  22.5 20.9 %collective-permute-start.6 = (f32[512,256]{1,0:T(8,128)S(1)}, f32[512,256]{1,0:T(8,128)}, u32[]{:S(2)}, u32[]{:S(2)}) collective-permute-start(f32[512,256]{1,0:T(8,128)S(1)} %collective-permute-done.3.refs_2_.guess), channel_id=1, source_target_pairs={{8,2},{2,8},{10,4},{4,10},{12,6},{6,12},{9,3},{3,9},{11,5},{5,11},... | collective-permute-start | bytes 1572872 | tf_op jit(solution)/shard_map/ppermute | solution.py:91
  23.9 19.5 %collective-permute-start.7 = (f32[512,256]{1,0:T(8,128)S(1)}, f32[512,256]{1,0:T(8,128)}, u32[]{:S(2)}, u32[]{:S(2)}) collective-permute-start(f32[512,256]{1,0:T(8,128)S(1)} %collective-permute-done.1.refs_0_.refs_1_), channel_id=1, source_target_pairs={{0,8},{8,0},{2,10},{10,2},{4,12},{12,4},{6,14},{14,6},{1,9},{9,1},... | collective-permute-start | bytes 1572872 | tf_op jit(solution)/shard_map/ppermute | solution.py:91
  33.7 9.7 %collective-permute-start.4 = (f32[512,256]{1,0:T(8,128)S(1)}, f32[512,256]{1,0:T(8,128)}, u32[]{:S(2)}, u32[]{:S(2)}) collective-permute-start(f32[512,256]{1,0:T(8,128)S(1)} %collective-permute-done.1.refs_0_.refs_1_), channel_id=1, source_target_pairs={{8,2},{2,8},{10,4},{4,10},{12,6},{6,12},{9,3},{3,9},{11,5},{5,11},... | collective-permute-start | bytes 1572872 | tf_op jit(solution)/shard_map/ppermute | solution.py:91
  63.2 13.1 %collective-permute-start.16 = (f32[512,256]{1,0:T(8,128)}, f32[512,256]{1,0:T(8,128)S(1)}, u32[]{:S(2)}, u32[]{:S(2)}) collective-permute-start(f32[512,256]{1,0:T(8,128)} %shard_map.60.refs_2_.refs_8_), channel_id=1, source_target_pairs={{0,8},{8,0},{2,10},{10,2},{4,12},{12,4},{6,14},{14,6},{1,9},{9,1},... | collective-permute-start | bytes 1572872 | tf_op jit(solution)/shard_map/ppermute | solution.py:91
  72.3 25.8 %collective-permute-start.21 = (f32[512,256]{1,0:T(8,128)S(1)}, f32[512,256]{1,0:T(8,128)S(1)}, u32[]{:S(2)}, u32[]{:S(2)}) collective-permute-start(f32[512,256]{1,0:T(8,128)S(1)} %copy-done.3), channel_id=1, source_target_pairs={{0,8},{8,0},{2,10},{10,2},{4,12},{12,4},{6,14},{14,6},{1,9},{9,1},... | collective-permute-start | bytes 1572872 | tf_op jit(solution)/shard_map/ppermute | solution.py:91
  75.6 22.5 %collective-permute-start.20 = (f32[512,256]{1,0:T(8,128)S(1)}, f32[512,256]{1,0:T(8,128)S(1)}, u32[]{:S(2)}, u32[]{:S(2)}) collective-permute-start(f32[512,256]{1,0:T(8,128)S(1)} %copy-done.3), channel_id=1, source_target_pairs={{8,2},{2,8},{10,4},{4,10},{12,6},{6,12},{9,3},{3,9},{11,5},{5,11},... | collective-permute-start | bytes 1572872 | tf_op jit(solution)/shard_map/ppermute | solution.py:91
  106.1 26.0 %collective-permute-start.29 = (f32[512,256]{1,0:T(8,128)S(1)}, f32[512,256]{1,0:T(8,128)S(1)}, u32[]{:S(2)}, u32[]{:S(2)}) collective-permute-start(f32[512,256]{1,0:T(8,128)S(1)} %copy-done.4), channel_id=1, source_target_pairs={{0,8},{8,0},{2,10},{10,2},{4,12},{12,4},{6,14},{14,6},{1,9},{9,1},... | collective-permute-start | bytes 1572872 | tf_op jit(solution)/shard_map/ppermute | solution.py:91
  109.4 22.7 %collective-permute-start.28 = (f32[512,256]{1,0:T(8,128)S(1)}, f32[512,256]{1,0:T(8,128)S(1)}, u32[]{:S(2)}, u32[]{:S(2)}) collective-permute-start(f32[512,256]{1,0:T(8,128)S(1)} %copy-done.4), channel_id=1, source_target_pairs={{8,2},{2,8},{10,4},{4,10},{12,6},{6,12},{9,3},{3,9},{11,5},{5,11},... | collective-permute-start | bytes 1572872 | tf_op jit(solution)/shard_map/ppermute | solution.py:91
  138.4 9.2 %collective-permute-start.32 = (f32[512,256]{1,0:T(8,128)}, f32[512,256]{1,0:T(8,128)S(1)}, u32[]{:S(2)}, u32[]{:S(2)}) collective-permute-start(f32[512,256]{1,0:T(8,128)} %get-tuple-element.26.refs_2_.image), channel_id=1, source_target_pairs={{0,8},{8,0},{2,10},{10,2},{4,12},{12,4},{6,14},{14,6},{1,9},{9,1},... | collective-permute-start | bytes 1572872 | tf_op jit(solution)/shard_map/ppermute | solution.py:91
  138.4 9.2 %collective-permute-start.31 = (f32[512,256]{1,0:T(8,128)}, f32[512,256]{1,0:T(8,128)S(1)}, u32[]{:S(2)}, u32[]{:S(2)}) collective-permute-start(f32[512,256]{1,0:T(8,128)} %get-tuple-element.26.refs_2_.image), channel_id=1, source_target_pairs={{8,2},{2,8},{10,4},{4,10},{12,6},{6,12},{9,3},{3,9},{11,5},{5,11},... | collective-permute-start | bytes 1572872 | tf_op jit(solution)/shard_map/ppermute | solution.py:91
  143.6 27.2 %collective-permute-start.39 = (f32[512,256]{1,0:T(8,128)}, f32[512,256]{1,0:T(8,128)S(1)}, u32[]{:S(2)}, u32[]{:S(2)}) collective-permute-start(f32[512,256]{1,0:T(8,128)} %get-tuple-element.28.refs_2_.image), channel_id=1, source_target_pairs={{0,8},{8,0},{2,10},{10,2},{4,12},{12,4},{6,14},{14,6},{1,9},{9,1},... | collective-permute-start | bytes 1572872 | tf_op jit(solution)/shard_map/ppermute | solution.py:91
  146.9 23.9 %collective-permute-start.38 = (f32[512,256]{1,0:T(8,128)}, f32[512,256]{1,0:T(8,128)S(1)}, u32[]{:S(2)}, u32[]{:S(2)}) collective-permute-start(f32[512,256]{1,0:T(8,128)} %get-tuple-element.28.refs_2_.image), channel_id=1, source_target_pairs={{8,2},{2,8},{10,4},{4,10},{12,6},{6,12},{9,3},{3,9},{11,5},{5,11},... | collective-permute-start | bytes 1572872 | tf_op jit(solution)/shard_map/ppermute | solution.py:91
  162.6 34.0 %collective-permute-start.22 = (f32[512,256]{1,0:T(8,128)}, f32[512,256]{1,0:T(8,128)S(1)}, u32[]{:S(2)}, u32[]{:S(2)}) collective-permute-start(f32[512,256]{1,0:T(8,128)} %get-tuple-element.18), channel_id=1, source_target_pairs={{0,0},{1,8},{2,2},{3,10},{4,4},{5,12},{6,6},{7,14},{8,1},{9,9},{10... | collective-permute-start | bytes 1572872 | tf_op jit(solution)/shard_map/ppermute | solution.py:91
  164.3 32.4 %collective-permute-start.30 = (f32[512,256]{1,0:T(8,128)}, f32[512,256]{1,0:T(8,128)S(1)}, u32[]{:S(2)}, u32[]{:S(2)}) collective-permute-start(f32[512,256]{1,0:T(8,128)} %get-tuple-element.24), channel_id=1, source_target_pairs={{0,0},{1,8},{2,2},{3,10},{4,4},{5,12},{6,6},{7,14},{8,1},{9,9},{10... | collective-permute-start | bytes 1572872 | tf_op jit(solution)/shard_map/ppermute | solution.py:91
  169.1 27.5 %collective-permute-start.36 = (f32[512,256]{1,0:T(8,128)}, f32[512,256]{1,0:T(8,128)S(1)}, u32[]{:S(2)}, u32[]{:S(2)}) collective-permute-start(f32[512,256]{1,0:T(8,128)} %shard_map.66), channel_id=1, source_target_pairs={{0,0},{1,8},{2,2},{3,10},{4,4},{5,12},{6,6},{7,14},{8,1},{9,9},{10... | collective-permute-start | bytes 1572872 | tf_op jit(solution)/shard_map/ppermute | solution.py:91
  192.8 17.8 %collective-permute-start.43 = (f32[512,256]{1,0:T(8,128)}, f32[512,256]{1,0:T(8,128)S(1)}, u32[]{:S(2)}, u32[]{:S(2)}) collective-permute-start(f32[512,256]{1,0:T(8,128)} %shard_map.69), channel_id=1, source_target_pairs={{0,8},{8,9},{2,10},{10,11},{4,12},{12,13},{6,14},{14,15},{1,16},{9... | collective-permute-start | bytes 1572872 | tf_op jit(solution)/shard_map/ppermute | solution.py:91
  194.7 25.3 %collective-permute-start.37 = (f32[512,256]{1,0:T(8,128)S(1)}, f32[512,256]{1,0:T(8,128)S(1)}, u32[]{:S(2)}, u32[]{:S(2)}) collective-permute-start(f32[512,256]{1,0:T(8,128)S(1)} %copy-done.20), channel_id=1, source_target_pairs={{0,8},{8,9},{2,10},{10,11},{4,12},{12,13},{6,14},{14,15},{1,16},{9... | collective-permute-start | bytes 1572872 | tf_op jit(solution)/shard_map/ppermute | solution.py:91
  (46 other events, 318.9 us)

commit v2 on v1

--- a/solution.py
+++ b/solution.py
@@ -27,6 +27,7 @@
 ROWS = 16
 KINDS = 16
 LANES = 128
+SCOPED = 8 * 2**20
 
 
 def sweep_weight(row, column):
@@ -264,12 +265,17 @@
 
 def call(kernel, shapes, *args, scalars=0):
     single = not isinstance(shapes, list)
-    outs = [jax.ShapeDtypeStruct(shape, jnp.float32) for shape in ([shapes] if single else shapes)]
+    outs = [pltpu.VMEM(shape, jnp.float32) for shape in ([shapes] if single else shapes)]
+    args = [
+        arg if index < scalars else pltpu.with_memory_space_constraint(arg, pltpu.VMEM)
+        for index, arg in enumerate(args)
+    ]
     found = pl.pallas_call(
         kernel,
         out_shape=outs,
         in_specs=[SMEM] * scalars + [VMEM] * (len(args) - scalars),
         out_specs=[VMEM] * len(outs),
+        compiler_params=pltpu.CompilerParams(vmem_limit_bytes=SCOPED),
     )(*args)
     return found[0] if single else found
 

time: 222 us -> 187 us (0.84)
  Pallas kernels: 49 us -> 16.7 us
  starting transfers between devices: 110 us -> 119 us
  local copies, waits for them, and re-layouts: 10.3 us -> 2.3 us
  other arithmetic: 7.51 us -> 3.76 us
    pallas_call x12, Pallas kernels: 49 us -> 16.7 us  [call(): pl.pallas_call(kernel, out_shape=outs, in_specs=[SMEM] * scalars + [VMEM]...]
    ppermute x44, starting transfers between devices: 110 us -> 119 us  [move(): return lax.ppermute(value, AXES, perm)]
    unnamed x52 -> x26, local copies, waits for them, and re-layouts: 8.84 us -> 0.85 us
    add x12, other arithmetic: 5.2 us -> 0.04 us  [gather(): message = sum([move(message, perm) for perm in turns], message)]
  transfers between devices with their start and end apart: 44 -> 44, of which waited for: 14 -> 15; matrix products, arithmetic and copies ran while one was open for 4% -> 2% of each run, Pallas kernels for 13% -> 5%
where the time goes in v2:
time: 187 us; the launch traced here: 185 us
  starting transfers between devices  119 us (64%)
  waiting for transfers between devices  42.6 us (23%)
  Pallas kernels  16.7 us (9%)
  other arithmetic  3.76 us (2%)
  local copies, waits for them, and re-layouts  2.3 us (1%)
    ppermute x44, starting transfers between devices, move(): return lax.ppermute(value, AXES, perm)  119 us
    ppermute x44, waiting for transfers between devices, move(): return lax.ppermute(value, AXES, perm)  42.6 us
    pallas_call x12, Pallas kernels, call(): pl.pallas_call(kernel, out_shape=outs, in_specs=[SMEM] * scalars + [VMEM]...  16.7 us
  transfers between devices with their start and end apart: 44, of which 15 were waited for; matrix products, arithmetic and copies ran while one was open for 2% of the time, Pallas kernels for 5%

profile of v2, /device:TPU:2, one launch (start us, length us, event | category | flops | bytes accessed | tf_op | source)
XLA Modules:
  0.0 185.4 jit_solution(14091904047185259331)
XLA Ops:
  7.6 9.3 %collective-permute-start.12 = (f32[512,256]{1,0:T(8,128)S(1)}, f32[512,256]{1,0:T(8,128)S(1)}, u32[]{:S(2)}, u32[]{:S(2)}) collective-permute-start(f32[512,256]{1,0:T(8,128)S(1)} %collective-permute-done.10.kappa), channel_id=1, source_target_pairs={{0,8},{8,0},{2,10},{10,2},{4,12},{12,4},{6,14},{14,6},{1,9},{9,1},... | collective-permute-start | bytes 1572872 | tf_op jit(solution)/shard_map/ppermute | solution.py:92
  17.6 4.9 %collective-permute-start.9 = (f32[512,256]{1,0:T(8,128)S(1)}, f32[512,256]{1,0:T(8,128)S(1)}, u32[]{:S(2)}, u32[]{:S(2)}) collective-permute-start(f32[512,256]{1,0:T(8,128)S(1)} %collective-permute-done.3.refs_2_.guess), channel_id=1, source_target_pairs={{0,8},{8,0},{2,10},{10,2},{4,12},{12,4},{6,14},{14,6},{1,9},{9,1},... | collective-permute-start | bytes 1572872 | tf_op jit(solution)/shard_map/ppermute | solution.py:92
  23.2 10.5 %collective-permute-start.7 = (f32[512,256]{1,0:T(8,128)S(1)}, f32[512,256]{1,0:T(8,128)S(1)}, u32[]{:S(2)}, u32[]{:S(2)}) collective-permute-start(f32[512,256]{1,0:T(8,128)S(1)} %collective-permute-done.1.refs_0_.refs_1_), channel_id=1, source_target_pairs={{0,8},{8,0},{2,10},{10,2},{4,12},{12,4},{6,14},{14,6},{1,9},{9,1},... | collective-permute-start | bytes 1572872 | tf_op jit(solution)/shard_map/ppermute | solution.py:92
  34.4 3.3 %collective-permute-start.8 = (f32[512,256]{1,0:T(8,128)S(1)}, f32[512,256]{1,0:T(8,128)S(1)}, u32[]{:S(2)}, u32[]{:S(2)}) collective-permute-start(f32[512,256]{1,0:T(8,128)S(1)} %collective-permute-done.2.refs_1_), channel_id=1, source_target_pairs={{0,8},{8,0},{2,10},{10,2},{4,12},{12,4},{6,14},{14,6},{1,9},{9,1},... | collective-permute-start | bytes 1572872 | tf_op jit(solution)/shard_map/ppermute | solution.py:92
  42.3 10.9 %collective-permute-start.14 = (f32[512,256]{1,0:T(8,128)S(1)}, f32[512,256]{1,0:T(8,128)S(1)}, u32[]{:S(2)}, u32[]{:S(2)}) collective-permute-start(f32[512,256]{1,0:T(8,128)S(1)} %get-tuple-element.16.refs_0_.refs_1_.refs_5_), channel_id=1, source_target_pairs={{0,8},{8,0},{2,10},{10,2},{4,12},{12,4},{6,14},{14,6},{1,9},{9,1},... | collective-permute-start | bytes 1572872 | tf_op jit(solution)/shard_map/ppermute | solution.py:92
  56.0 9.1 %collective-permute-start.16 = (f32[512,256]{1,0:T(8,128)}, f32[512,256]{1,0:T(8,128)}, u32[]{:S(2)}, u32[]{:S(2)}) collective-permute-start(f32[512,256]{1,0:T(8,128)} %shard_map.60.refs_2_.refs_8_), channel_id=1, source_target_pairs={{0,8},{8,0},{2,10},{10,2},{4,12},{12,4},{6,14},{14,6},{1,9},{9,1},... | collective-permute-start | bytes 1572872 | tf_op jit(solution)/shard_map/ppermute | solution.py:92
  66.5 2.6 %collective-permute-start.21 = (f32[512,256]{1,0:T(8,128)}, f32[512,256]{1,0:T(8,128)}, u32[]{:S(2)}, u32[]{:S(2)}) collective-permute-start(f32[512,256]{1,0:T(8,128)} %get-tuple-element.17.refs_2_.refs_1_), channel_id=1, source_target_pairs={{0,8},{8,0},{2,10},{10,2},{4,12},{12,4},{6,14},{14,6},{1,9},{9,1},... | collective-permute-start | bytes 1572872 | tf_op jit(solution)/shard_map/ppermute | solution.py:92
  70.6 2.4 %shard_map.61 = f32[16,128]{1,0:T(8,128)S(1)} custom-call(s32[1]{0:T(128)} %bitcast.refs_0_, f32[512,256]{1,0:T(8,128)S(1)} %get-tuple-element.16.refs_0_.refs_1_.refs_5_, f32[512,256]{1,0:T(8,128)} %shard_map.60.refs_2_.refs_8_, f32[512,256]{1,0:T(8,128)} %collective-permute-done.15.refs_3_.refs_9_, f32[512,256]{1,0:T(8,128)} %collective-permute-done.16.refs_4_.refs_10_, ...), custom_call_target="tpu_custom_call" | custom-call | tf_op jit(solution)/shard_map/pallas_call | solution.py:273
  73.0 5.6 %collective-permute-start.17 = (f32[16,128]{1,0:T(8,128)S(1)}, f32[16,128]{1,0:T(8,128)S(1)}, u32[]{:S(2)}, u32[]{:S(2)}) collective-permute-start(f32[16,128]{1,0:T(8,128)S(1)} %shard_map.61), channel_id=1, source_target_pairs={{0,8},{8,0},{2,10},{10,2},{4,12},{12,4},{6,14},{14,6},{1,9},{9,1},... | collective-permute-start | bytes 24584 | tf_op jit(solution)/shard_map/ppermute | solution.py:92
  83.1 3.0 %collective-permute-start.19 = (f32[16,128]{1,0:T(8,128)S(1)}, f32[16,128]{1,0:T(8,128)S(1)}, u32[]{:S(2)}, u32[]{:S(2)}) collective-permute-start(f32[16,128]{1,0:T(8,128)S(1)} %add.47), channel_id=1, source_target_pairs={{0,4},{8,12},{2,6},{10,14},{4,0},{12,8},{6,2},{14,10},{1,5},{9,13}... | collective-permute-start | bytes 24584 | tf_op jit(solution)/shard_map/ppermute | solution.py:92
  87.8 3.2 %shard_map.62 = (f32[512,256]{1,0:T(8,128)}, f32[512,256]{1,0:T(8,128)S(1)}, f32[512,256]{1,0:T(8,128)S(1)}, f32[512,256]{1,0:T(8,128)S(1)}, f32[512,256]{1,0:T(8,128)S(1)}) custom-call(f32[16,128]{1,0:T(8,128)S(1)} %add.48.refs_0_, f32[512,256]{1,0:T(8,128)S(1)} %copy-done.11, f32[512,256]{1,0:T(8,128)} %get-tuple-element.17.refs_2_.refs_1_, ...), custom_call_target="tpu_custom_call" | custom-call | tf_op jit(solution)/shard_map/pallas_call | solution.py:273
  91.7 3.3 %collective-permute-start.29 = (f32[512,256]{1,0:T(8,128)S(1)}, f32[512,256]{1,0:T(8,128)S(1)}, u32[]{:S(2)}, u32[]{:S(2)}) collective-permute-start(f32[512,256]{1,0:T(8,128)S(1)} %copy-done.7), channel_id=1, source_target_pairs={{0,8},{8,0},{2,10},{10,2},{4,12},{12,4},{6,14},{14,6},{1,9},{9,1},... | collective-permute-start | bytes 1572872 | tf_op jit(solution)/shard_map/ppermute | solution.py:92
  96.7 6.3 %collective-permute-start.25 = (f32[16,128]{1,0:T(8,128)S(1)}, f32[16,128]{1,0:T(8,128)S(1)}, u32[]{:S(2)}, u32[]{:S(2)}) collective-permute-start(f32[16,128]{1,0:T(8,128)S(1)} %shard_map.63), channel_id=1, source_target_pairs={{0,8},{8,0},{2,10},{10,2},{4,12},{12,4},{6,14},{14,6},{1,9},{9,1},... | collective-permute-start | bytes 24584 | tf_op jit(solution)/shard_map/ppermute | solution.py:92
  108.0 2.9 %collective-permute-start.27 = (f32[16,128]{1,0:T(8,128)S(1)}, f32[16,128]{1,0:T(8,128)S(1)}, u32[]{:S(2)}, u32[]{:S(2)}) collective-permute-start(f32[16,128]{1,0:T(8,128)S(1)} %add.50), channel_id=1, source_target_pairs={{0,4},{8,12},{2,6},{10,14},{4,0},{12,8},{6,2},{14,10},{1,5},{9,13}... | collective-permute-start | bytes 24584 | tf_op jit(solution)/shard_map/ppermute | solution.py:92
  116.6 3.1 %collective-permute-start.39 = (f32[512,256]{1,0:T(8,128)S(1)}, f32[512,256]{1,0:T(8,128)S(1)}, u32[]{:S(2)}, u32[]{:S(2)}) collective-permute-start(f32[512,256]{1,0:T(8,128)S(1)} %get-tuple-element.28.refs_2_.image), channel_id=1, source_target_pairs={{0,8},{8,0},{2,10},{10,2},{4,12},{12,4},{6,14},{14,6},{1,9},{9,1},... | collective-permute-start | bytes 1572872 | tf_op jit(solution)/shard_map/ppermute | solution.py:92
  121.5 4.4 %collective-permute-start.33 = (f32[16,128]{1,0:T(8,128)S(1)}, f32[16,128]{1,0:T(8,128)S(1)}, u32[]{:S(2)}, u32[]{:S(2)}) collective-permute-start(f32[16,128]{1,0:T(8,128)S(1)} %shard_map.65), channel_id=1, source_target_pairs={{0,8},{8,0},{2,10},{10,2},{4,12},{12,4},{6,14},{14,6},{1,9},{9,1},... | collective-permute-start | bytes 24584 | tf_op jit(solution)/shard_map/ppermute | solution.py:92
  130.9 2.9 %collective-permute-start.35 = (f32[16,128]{1,0:T(8,128)S(1)}, f32[16,128]{1,0:T(8,128)S(1)}, u32[]{:S(2)}, u32[]{:S(2)}) collective-permute-start(f32[16,128]{1,0:T(8,128)S(1)} %add.53), channel_id=1, source_target_pairs={{0,4},{8,12},{2,6},{10,14},{4,0},{12,8},{6,2},{14,10},{1,5},{9,13}... | collective-permute-start | bytes 24584 | tf_op jit(solution)/shard_map/ppermute | solution.py:92
  133.8 5.4 %collective-permute-start.22 = (f32[512,256]{1,0:T(8,128)}, f32[512,256]{1,0:T(8,128)}, u32[]{:S(2)}, u32[]{:S(2)}) collective-permute-start(f32[512,256]{1,0:T(8,128)} %get-tuple-element.18), channel_id=1, source_target_pairs={{0,0},{1,8},{2,2},{3,10},{4,4},{5,12},{6,6},{7,14},{8,1},{9,9},{10... | collective-permute-start | bytes 1572872 | tf_op jit(solution)/shard_map/ppermute | solution.py:92
  139.2 5.4 %collective-permute-start.30 = (f32[512,256]{1,0:T(8,128)}, f32[512,256]{1,0:T(8,128)}, u32[]{:S(2)}, u32[]{:S(2)}) collective-permute-start(f32[512,256]{1,0:T(8,128)} %get-tuple-element.24), channel_id=1, source_target_pairs={{0,0},{1,8},{2,2},{3,10},{4,4},{5,12},{6,6},{7,14},{8,1},{9,9},{10... | collective-permute-start | bytes 1572872 | tf_op jit(solution)/shard_map/ppermute | solution.py:92
  148.6 3.6 %collective-permute-done.41 = f32[16,128]{1,0:T(8,128)S(1)} collective-permute-done((f32[16,128]{1,0:T(8,128)S(1)}, f32[16,128]{1,0:T(8,128)S(1)}, u32[]{:S(2)}, u32[]{:S(2)}) %collective-permute-start.41) | collective-permute-done | bytes 8224 | tf_op jit(solution)/shard_map/ppermute | solution.py:92
  152.2 4.5 %collective-permute-done.42 = f32[16,128]{1,0:T(8,128)S(1)} collective-permute-done((f32[16,128]{1,0:T(8,128)S(1)}, f32[16,128]{1,0:T(8,128)S(1)}, u32[]{:S(2)}, u32[]{:S(2)}) %collective-permute-start.42) | collective-permute-done | bytes 8224 | tf_op jit(solution)/shard_map/ppermute | solution.py:92
  161.1 2.7 %maximum_bitcast_fusion = f32[1,3,1,512,256]{4,3,2,1,0:T(8,128)} fusion(f32[1,512,256]{2,1,0:T(8,128)} %bitcast.8, f32[1,512,256]{2,1,0:T(8,128)} %bitcast.7, f32[1,512,256]{2,1,0:T(8,128)} %bitcast.6), kind=kLoop, calls=%fused_computation | loop fusion | flops 786432 | bytes 3145728
  163.7 11.0 %collective-permute-done.43 = f32[512,256]{1,0:T(8,128)S(1)} collective-permute-done((f32[512,256]{1,0:T(8,128)S(1)}, f32[512,256]{1,0:T(8,128)S(1)}, u32[]{:S(2)}, u32[]{:S(2)}) %collective-permute-start.43) | collective-permute-done | bytes 524320 | tf_op jit(solution)/shard_map/ppermute | solution.py:92
  174.7 9.6 %collective-permute-done.37 = f32[512,256]{1,0:T(8,128)S(1)} collective-permute-done((f32[512,256]{1,0:T(8,128)S(1)}, f32[512,256]{1,0:T(8,128)S(1)}, u32[]{:S(2)}, u32[]{:S(2)}) %collective-permute-start.37) | collective-permute-done | bytes 524320 | tf_op jit(solution)/shard_map/ppermute | solution.py:92
  (117 shorter events, 54.5 us)
Async XLA Ops:
  2.3 14.6 %collective-permute-start = (f32[512,256]{1,0:T(8,128)}, f32[512,256]{1,0:T(8,128)S(1)}, u32[]{:S(2)}, u32[]{:S(2)}) collective-permute-start(f32[512,256]{1,0:T(8,128)} %bitcast.20), channel_id=1, source_target_pairs={{0,0},{1,8},{2,2},{3,10},{4,4},{5,12},{6,6},{7,14},{8,1},{9,9},{10... | collective-permute-start | bytes 1572872 | tf_op jit(solution)/shard_map/ppermute | solution.py:92
  5.5 12.1 %collective-permute-start.3 = (f32[512,256]{1,0:T(8,128)S(1)}, f32[512,256]{1,0:T(8,128)S(1)}, u32[]{:S(2)}, u32[]{:S(2)}) collective-permute-start(f32[512,256]{1,0:T(8,128)S(1)} %get-tuple-element.32), channel_id=1, source_target_pairs={{0,0},{1,8},{2,2},{3,10},{4,4},{5,12},{6,6},{7,14},{8,1},{9,9},{10... | collective-permute-start | bytes 1572872 | tf_op jit(solution)/shard_map/ppermute | solution.py:92
  6.2 16.3 %collective-permute-start.1 = (f32[512,256]{1,0:T(8,128)S(1)}, f32[512,256]{1,0:T(8,128)S(1)}, u32[]{:S(2)}, u32[]{:S(2)}) collective-permute-start(f32[512,256]{1,0:T(8,128)S(1)} %get-tuple-element.33), channel_id=1, source_target_pairs={{0,0},{1,8},{2,2},{3,10},{4,4},{5,12},{6,6},{7,14},{8,1},{9,9},{10... | collective-permute-start | bytes 1572872 | tf_op jit(solution)/shard_map/ppermute | solution.py:92
  6.9 16.3 %collective-permute-start.2 = (f32[512,256]{1,0:T(8,128)S(1)}, f32[512,256]{1,0:T(8,128)S(1)}, u32[]{:S(2)}, u32[]{:S(2)}) collective-permute-start(f32[512,256]{1,0:T(8,128)S(1)} %get-tuple-element.34), channel_id=1, source_target_pairs={{0,0},{1,8},{2,2},{3,10},{4,4},{5,12},{6,6},{7,14},{8,1},{9,9},{10... | collective-permute-start | bytes 1572872 | tf_op jit(solution)/shard_map/ppermute | solution.py:92
  7.6 26.1 %collective-permute-start.12 = (f32[512,256]{1,0:T(8,128)S(1)}, f32[512,256]{1,0:T(8,128)S(1)}, u32[]{:S(2)}, u32[]{:S(2)}) collective-permute-start(f32[512,256]{1,0:T(8,128)S(1)} %collective-permute-done.10.kappa), channel_id=1, source_target_pairs={{0,8},{8,0},{2,10},{10,2},{4,12},{12,4},{6,14},{14,6},{1,9},{9,1},... | collective-permute-start | bytes 1572872 | tf_op jit(solution)/shard_map/ppermute | solution.py:92
  16.9 17.5 %collective-permute-start.11 = (f32[512,256]{1,0:T(8,128)S(1)}, f32[512,256]{1,0:T(8,128)S(1)}, u32[]{:S(2)}, u32[]{:S(2)}) collective-permute-start(f32[512,256]{1,0:T(8,128)S(1)} %collective-permute-done.10.kappa), channel_id=1, source_target_pairs={{8,2},{2,8},{10,4},{4,10},{12,6},{6,12},{9,3},{3,9},{11,5},{5,11},... | collective-permute-start | bytes 1572872 | tf_op jit(solution)/shard_map/ppermute | solution.py:92
  17.6 20.1 %collective-permute-start.9 = (f32[512,256]{1,0:T(8,128)S(1)}, f32[512,256]{1,0:T(8,128)S(1)}, u32[]{:S(2)}, u32[]{:S(2)}) collective-permute-start(f32[512,256]{1,0:T(8,128)S(1)} %collective-permute-done.3.refs_2_.guess), channel_id=1, source_target_pairs={{0,8},{8,0},{2,10},{10,2},{4,12},{12,4},{6,14},{14,6},{1,9},{9,1},... | collective-permute-start | bytes 1572872 | tf_op jit(solution)/shard_map/ppermute | solution.py:92
  22.5 16.4 %collective-permute-start.6 = (f32[512,256]{1,0:T(8,128)S(1)}, f32[512,256]{1,0:T(8,128)S(1)}, u32[]{:S(2)}, u32[]{:S(2)}) collective-permute-start(f32[512,256]{1,0:T(8,128)S(1)} %collective-permute-done.3.refs_2_.guess), channel_id=1, source_target_pairs={{8,2},{2,8},{10,4},{4,10},{12,6},{6,12},{9,3},{3,9},{11,5},{5,11},... | collective-permute-start | bytes 1572872 | tf_op jit(solution)/shard_map/ppermute | solution.py:92
  23.2 15.7 %collective-permute-start.7 = (f32[512,256]{1,0:T(8,128)S(1)}, f32[512,256]{1,0:T(8,128)S(1)}, u32[]{:S(2)}, u32[]{:S(2)}) collective-permute-start(f32[512,256]{1,0:T(8,128)S(1)} %collective-permute-done.1.refs_0_.refs_1_), channel_id=1, source_target_pairs={{0,8},{8,0},{2,10},{10,2},{4,12},{12,4},{6,14},{14,6},{1,9},{9,1},... | collective-permute-start | bytes 1572872 | tf_op jit(solution)/shard_map/ppermute | solution.py:92
  42.3 12.4 %collective-permute-start.14 = (f32[512,256]{1,0:T(8,128)S(1)}, f32[512,256]{1,0:T(8,128)S(1)}, u32[]{:S(2)}, u32[]{:S(2)}) collective-permute-start(f32[512,256]{1,0:T(8,128)S(1)} %get-tuple-element.16.refs_0_.refs_1_.refs_5_), channel_id=1, source_target_pairs={{0,8},{8,0},{2,10},{10,2},{4,12},{12,4},{6,14},{14,6},{1,9},{9,1},... | collective-permute-start | bytes 1572872 | tf_op jit(solution)/shard_map/ppermute | solution.py:92
  56.0 14.6 %collective-permute-start.16 = (f32[512,256]{1,0:T(8,128)}, f32[512,256]{1,0:T(8,128)}, u32[]{:S(2)}, u32[]{:S(2)}) collective-permute-start(f32[512,256]{1,0:T(8,128)} %shard_map.60.refs_2_.refs_8_), channel_id=1, source_target_pairs={{0,8},{8,0},{2,10},{10,2},{4,12},{12,4},{6,14},{14,6},{1,9},{9,1},... | collective-permute-start | bytes 1572872 | tf_op jit(solution)/shard_map/ppermute | solution.py:92
  66.5 21.3 %collective-permute-start.21 = (f32[512,256]{1,0:T(8,128)}, f32[512,256]{1,0:T(8,128)}, u32[]{:S(2)}, u32[]{:S(2)}) collective-permute-start(f32[512,256]{1,0:T(8,128)} %get-tuple-element.17.refs_2_.refs_1_), channel_id=1, source_target_pairs={{0,8},{8,0},{2,10},{10,2},{4,12},{12,4},{6,14},{14,6},{1,9},{9,1},... | collective-permute-start | bytes 1572872 | tf_op jit(solution)/shard_map/ppermute | solution.py:92
  69.1 18.7 %collective-permute-start.20 = (f32[512,256]{1,0:T(8,128)}, f32[512,256]{1,0:T(8,128)}, u32[]{:S(2)}, u32[]{:S(2)}) collective-permute-start(f32[512,256]{1,0:T(8,128)} %get-tuple-element.17.refs_2_.refs_1_), channel_id=1, source_target_pairs={{8,2},{2,8},{10,4},{4,10},{12,6},{6,12},{9,3},{3,9},{11,5},{5,11},... | collective-permute-start | bytes 1572872 | tf_op jit(solution)/shard_map/ppermute | solution.py:92
  91.7 20.8 %collective-permute-start.29 = (f32[512,256]{1,0:T(8,128)S(1)}, f32[512,256]{1,0:T(8,128)S(1)}, u32[]{:S(2)}, u32[]{:S(2)}) collective-permute-start(f32[512,256]{1,0:T(8,128)S(1)} %copy-done.7), channel_id=1, source_target_pairs={{0,8},{8,0},{2,10},{10,2},{4,12},{12,4},{6,14},{14,6},{1,9},{9,1},... | collective-permute-start | bytes 1572872 | tf_op jit(solution)/shard_map/ppermute | solution.py:92
  95.0 17.5 %collective-permute-start.28 = (f32[512,256]{1,0:T(8,128)S(1)}, f32[512,256]{1,0:T(8,128)S(1)}, u32[]{:S(2)}, u32[]{:S(2)}) collective-permute-start(f32[512,256]{1,0:T(8,128)S(1)} %copy-done.7), channel_id=1, source_target_pairs={{8,2},{2,8},{10,4},{4,10},{12,6},{6,12},{9,3},{3,9},{11,5},{5,11},... | collective-permute-start | bytes 1572872 | tf_op jit(solution)/shard_map/ppermute | solution.py:92
  96.7 7.1 %collective-permute-start.25 = (f32[16,128]{1,0:T(8,128)S(1)}, f32[16,128]{1,0:T(8,128)S(1)}, u32[]{:S(2)}, u32[]{:S(2)}) collective-permute-start(f32[16,128]{1,0:T(8,128)S(1)} %shard_map.63), channel_id=1, source_target_pairs={{0,8},{8,0},{2,10},{10,2},{4,12},{12,4},{6,14},{14,6},{1,9},{9,1},... | collective-permute-start | bytes 24584 | tf_op jit(solution)/shard_map/ppermute | solution.py:92
  116.6 29.8 %collective-permute-start.39 = (f32[512,256]{1,0:T(8,128)S(1)}, f32[512,256]{1,0:T(8,128)S(1)}, u32[]{:S(2)}, u32[]{:S(2)}) collective-permute-start(f32[512,256]{1,0:T(8,128)S(1)} %get-tuple-element.28.refs_2_.image), channel_id=1, source_target_pairs={{0,8},{8,0},{2,10},{10,2},{4,12},{12,4},{6,14},{14,6},{1,9},{9,1},... | collective-permute-start | bytes 1572872 | tf_op jit(solution)/shard_map/ppermute | solution.py:92
  119.8 26.7 %collective-permute-start.38 = (f32[512,256]{1,0:T(8,128)S(1)}, f32[512,256]{1,0:T(8,128)S(1)}, u32[]{:S(2)}, u32[]{:S(2)}) collective-permute-start(f32[512,256]{1,0:T(8,128)S(1)} %get-tuple-element.28.refs_2_.image), channel_id=1, source_target_pairs={{8,2},{2,8},{10,4},{4,10},{12,6},{6,12},{9,3},{3,9},{11,5},{5,11},... | collective-permute-start | bytes 1572872 | tf_op jit(solution)/shard_map/ppermute | solution.py:92
  130.9 13.7 %collective-permute-start.35 = (f32[16,128]{1,0:T(8,128)S(1)}, f32[16,128]{1,0:T(8,128)S(1)}, u32[]{:S(2)}, u32[]{:S(2)}) collective-permute-start(f32[16,128]{1,0:T(8,128)S(1)} %add.53), channel_id=1, source_target_pairs={{0,4},{8,12},{2,6},{10,14},{4,0},{12,8},{6,2},{14,10},{1,5},{9,13}... | collective-permute-start | bytes 24584 | tf_op jit(solution)/shard_map/ppermute | solution.py:92
  133.8 27.2 %collective-permute-start.22 = (f32[512,256]{1,0:T(8,128)}, f32[512,256]{1,0:T(8,128)}, u32[]{:S(2)}, u32[]{:S(2)}) collective-permute-start(f32[512,256]{1,0:T(8,128)} %get-tuple-element.18), channel_id=1, source_target_pairs={{0,0},{1,8},{2,2},{3,10},{4,4},{5,12},{6,6},{7,14},{8,1},{9,9},{10... | collective-permute-start | bytes 1572872 | tf_op jit(solution)/shard_map/ppermute | solution.py:92
  139.2 21.9 %collective-permute-start.30 = (f32[512,256]{1,0:T(8,128)}, f32[512,256]{1,0:T(8,128)}, u32[]{:S(2)}, u32[]{:S(2)}) collective-permute-start(f32[512,256]{1,0:T(8,128)} %get-tuple-element.24), channel_id=1, source_target_pairs={{0,0},{1,8},{2,2},{3,10},{4,4},{5,12},{6,6},{7,14},{8,1},{9,9},{10... | collective-permute-start | bytes 1572872 | tf_op jit(solution)/shard_map/ppermute | solution.py:92
  145.0 16.1 %collective-permute-start.36 = (f32[512,256]{1,0:T(8,128)S(1)}, f32[512,256]{1,0:T(8,128)}, u32[]{:S(2)}, u32[]{:S(2)}) collective-permute-start(f32[512,256]{1,0:T(8,128)S(1)} %shard_map.66), channel_id=1, source_target_pairs={{0,0},{1,8},{2,2},{3,10},{4,4},{5,12},{6,6},{7,14},{8,1},{9,9},{10... | collective-permute-start | bytes 1572872 | tf_op jit(solution)/shard_map/ppermute | solution.py:92
  157.2 17.6 %collective-permute-start.43 = (f32[512,256]{1,0:T(8,128)S(1)}, f32[512,256]{1,0:T(8,128)S(1)}, u32[]{:S(2)}, u32[]{:S(2)}) collective-permute-start(f32[512,256]{1,0:T(8,128)S(1)} %shard_map.69), channel_id=1, source_target_pairs={{0,8},{8,9},{2,10},{10,11},{4,12},{12,13},{6,14},{14,15},{1,16},{9... | collective-permute-start | bytes 1572872 | tf_op jit(solution)/shard_map/ppermute | solution.py:92
  159.1 25.2 %collective-permute-start.37 = (f32[512,256]{1,0:T(8,128)S(1)}, f32[512,256]{1,0:T(8,128)S(1)}, u32[]{:S(2)}, u32[]{:S(2)}) collective-permute-start(f32[512,256]{1,0:T(8,128)S(1)} %shard_map.66), channel_id=1, source_target_pairs={{0,8},{8,9},{2,10},{10,11},{4,12},{12,13},{6,14},{14,15},{1,16},{9... | collective-permute-start | bytes 1572872 | tf_op jit(solution)/shard_map/ppermute | solution.py:92
  (33 other events, 267.6 us)
